TPU v7x, 32 devices: a whole 2x2x4 slice. The times are simulated.
32 devices in a mesh: dp: 8 (over z, y), group: 4 (over x, core).
Axes of the slice: x: 2, y: 2, z: 4, core: 2. Of those that a mesh axis runs over, the one named last changes fastest.
Arguments:
- rewards: bfloat16 [8192, 4096], P(('dp', 'group')), may hold values from -6 to 6
- values: bfloat16 [8192, 4096], P(('dp', 'group')), may hold values from -6 to 6
- lengths: int32 [8192], P(('dp', 'group')), may hold values from 1 to 4096
- decay_rate: float32 [8192], P(('dp', 'group')), may hold values from 3.8146973e-06 to 0.03125
- piece_dest: int32 [8, 8], P('dp'), may hold values from 0 to 7, each once within a row
- row_perm: int32 [64, 128], P(('dp', 'group')), may hold values from 0 to 127, each once within a row
- minibatch: int32 [8192], P(('dp', 'group')), may hold values from 0 to 63
Outputs:
- white_rewards: bfloat16 [8192, 4096], P(('dp', 'group'))
- white_advantage: bfloat16 [8192, 4096], P(('dp', 'group'))
Inputs may be any that keep to these rules, and one draw needn't show every extreme that they name: Each row of piece_dest names every index of dp once. Each row of row_perm names every number below 128 once.
All inputs are finite; a program needn't handle non-finite values.
Results may differ from a plain program's by a relative error of at most 0.0049.
Values may be sent and summed in bfloat16 or wider, within the bound.
A program may use at most 64 MiB of HBM per device.

v0:
```python
import functools

import jax
import jax.numpy as jnp
from jax import lax
from jax.experimental import pallas as pl
from jax.experimental.pallas import tpu as pltpu
from jax.sharding import PartitionSpec as P

MINIBATCHES = 64


HIGHEST = lax.Precision.HIGHEST


def discounted(rewards, values, lengths, decay_rate):
    rows_here, span = rewards.shape
    block = min(128, span)
    blocks_here = span // block
    position = jnp.arange(span, dtype=jnp.int32)
    is_valid = position[None, :] < lengths[:, None]
    next_valid = position[None, :] + 1 < lengths[:, None]
    per_step = jnp.exp(-decay_rate)
    value_f = values.astype(jnp.float32)
    value_next = jnp.concatenate([value_f[:, 1:], jnp.zeros((rows_here, 1), jnp.float32)], axis=1)
    td_error = (
        rewards.astype(jnp.float32)
        + per_step[:, None] * jnp.where(next_valid, value_next, 0.0)
        - value_f
    )
    td_error = jnp.where(is_valid, td_error, 0.0).reshape(rows_here, blocks_here, block)
    offset = jnp.arange(block, dtype=jnp.float32)
    lower_scale = jnp.exp(-decay_rate[:, None] * offset[None, :])
    upper_scale = jnp.exp(decay_rate[:, None] * offset[None, :])
    triangle = (offset[:, None] >= offset[None, :]).astype(jnp.float32)
    scaled = td_error * lower_scale[:, None, :]
    summed = jnp.einsum("rjk,kt->rjt", scaled, triangle, precision=HIGHEST)
    local_part = summed * upper_scale[:, None, :]
    heads = local_part[:, :, 0]
    block_step = jnp.exp(-decay_rate * block)

    def carry_step(carry, head):
        fresh = head + block_step * carry
        return (fresh, fresh)

    final_carry, starts = lax.scan(carry_step, jnp.zeros_like(decay_rate), heads.T, reverse=True)
    next_heads = jnp.concatenate([starts[1:].T, jnp.zeros((rows_here, 1), jnp.float32)], axis=1)
    reach = jnp.exp(-decay_rate[:, None] * (block - offset[None, :]))
    total = local_part + reach[:, None, :] * next_heads[:, :, None]
    return jnp.where(is_valid, total.reshape(rows_here, span), 0.0).astype(jnp.bfloat16)


def by_target(array, piece_dest):
    peers = piece_dest.shape[1]
    target = piece_dest[0]
    slots = jnp.arange(peers, dtype=jnp.int32)
    source_slot = jnp.sum(jnp.where(target[None, :] == slots[:, None], slots[None, :], 0), axis=1)
    pieces = array.reshape((peers, array.shape[0] // peers) + array.shape[1:])
    return jnp.take(pieces, source_slot, axis=0).reshape(array.shape)


def reorder(received, row_perm):
    blocks_here, block = row_perm.shape
    chooser = (row_perm[:, :, None] == jnp.arange(block, dtype=jnp.int32)[None, None, :]).astype(
        jnp.bfloat16
    )

    def permute_one(member):
        shaped = member.reshape(blocks_here, block, member.shape[-1])
        mixed = jnp.einsum("bim,bmc->bic", chooser, shaped, preferred_element_type=jnp.float32)
        return mixed.astype(jnp.bfloat16).reshape(member.shape)

    return tuple((permute_one(member) for member in received))


def whiten(rewards, advantage, lengths, minibatch):
    rows_here, span = rewards.shape
    position = jnp.arange(span, dtype=jnp.int32)
    is_valid = position[None, :] < lengths[:, None]
    counted = lengths.astype(jnp.float32)
    reward_f = jnp.where(is_valid, rewards.astype(jnp.float32), 0.0)
    advantage_f = jnp.where(is_valid, advantage.astype(jnp.float32), 0.0)
    member = (minibatch[:, None] == jnp.arange(MINIBATCHES, dtype=jnp.int32)[None, :]).astype(
        jnp.float32
    )
    row_terms = jnp.stack(
        [
            counted,
            jnp.sum(reward_f, axis=1),
            jnp.sum(advantage_f, axis=1),
            jnp.sum(reward_f * reward_f, axis=1),
            jnp.sum(advantage_f * advantage_f, axis=1),
        ],
        axis=1,
    )
    totals = lax.psum(jnp.dot(member.T, row_terms, precision=HIGHEST), ("dp", "group"))
    count = jnp.maximum(totals[:, 0], 1.0)
    means = totals[:, 1:3] / count[:, None]
    spreads = totals[:, 3:5] / count[:, None] - means * means
    row_means = jnp.dot(member, means, precision=HIGHEST)
    row_scale = jnp.dot(member, lax.rsqrt(spreads + 1e-05), precision=HIGHEST)
    white_rewards = jnp.where(is_valid, (reward_f - row_means[:, 0:1]) * row_scale[:, 0:1], 0.0)
    white_advantage = jnp.where(
        is_valid, (advantage_f - row_means[:, 1:2]) * row_scale[:, 1:2], 0.0
    )
    return (white_rewards.astype(jnp.bfloat16), white_advantage.astype(jnp.bfloat16))


def plain_local(rewards, values, lengths, decay_rate, piece_dest, row_perm, minibatch):
    blocks_here, block = row_perm.shape
    new_order = (jnp.arange(blocks_here, dtype=jnp.int32)[:, None] * block + row_perm).reshape(-1)
    per_row = jnp.stack([lengths.astype(jnp.float32), decay_rate], axis=1)
    moved_terms = lax.all_to_all(
        by_target(per_row, piece_dest), "dp", split_axis=0, concat_axis=0, tiled=True
    )
    moved_terms = jnp.take(moved_terms, new_order, axis=0)
    lengths_here = moved_terms[:, 0].astype(jnp.int32)
    rate_here = moved_terms[:, 1]
    moved_rewards, moved_second = reorder(
        (
            lax.all_to_all(
                by_target(rewards, piece_dest), "dp", split_axis=0, concat_axis=0, tiled=True
            ),
            lax.all_to_all(
                by_target(values, piece_dest), "dp", split_axis=0, concat_axis=0, tiled=True
            ),
        ),
        row_perm,
    )
    advantage = discounted(moved_rewards, moved_second, lengths_here, rate_here)
    return whiten(moved_rewards, advantage, lengths_here, minibatch)


F32 = jnp.float32
BF16 = jnp.bfloat16
LANES = 128
MESH = pl.DeviceIdType.MESH
NT = (((1,), (1,)), ((), ()))


def exchange_kernel(
    n_dp, n_group,
    rbuf, val_hbm, rate_ref, packed,
    white_r, white_a,
    out_r, out_a, out_st, out_ch,
    vbuf, abuf, rsend, asend, tri, lower, upper, lenb, bstep, carry,
    acc, tbuf, tstage, tsend, trecv, psend, precv, qsend, qrecv, tot,
    load_sem, own_sem, rs_sem, rr_sem, as_sem, ar_sem, ts_sem, tr_sem, ps_sem, pr_sem, qs_sem, qr_sem,
):
    rows, span = rbuf.shape
    blocks = out_ch.shape[0]
    piece = rows // n_dp
    wide = tri.shape[0]
    cuts = ((0, span // 2), (span // 2, 3 * span // 8), (7 * span // 8, span // 8))
    me = lax.axis_index("dp")
    mine = lax.axis_index("group")
    order = sorted(range(1, n_dp), key=lambda d: (abs(2 * d - n_dp), d))

    def dp_peer(d):
        return lax.rem(me + d, n_dp)

    def group_peer(d):
        return lax.rem(mine + d, n_group)

    quarter = rows // 4
    loads = []
    for part in range(4):
        at = pl.ds(part * quarter, quarter)
        loads.append(pltpu.make_async_copy(val_hbm.at[at], vbuf.at[at], load_sem.at[part]))
        loads[-1].start()

    def row_of(kind, b):
        return packed[kind * blocks + b : kind * blocks + b + 1, :].astype(F32)

    barrier = pltpu.get_barrier_semaphore()
    for d in range(1, n_dp):
        pl.semaphore_signal(barrier, inc=1, device_id=(dp_peer(d), mine), device_id_type=MESH)
    for d in range(1, n_group):
        pl.semaphore_signal(barrier, inc=1, device_id=(me, group_peer(d)), device_id_type=MESH)

    targets = [
        jnp.broadcast_to(row_of(3, 0)[:, p : p + 1], (piece, LANES)) for p in range(n_dp)
    ]

    def pick(d, source):
        k = jnp.full((piece, LANES), dp_peer(d), jnp.int32).astype(F32)
        weights = [(target == k).astype(F32).astype(source.dtype) for target in targets]
        for c in range(0, source.shape[1], LANES):
            at = slice(c, c + LANES)
            yield at, sum(source[p * piece : (p + 1) * piece, at] * weights[p] for p in range(n_dp))

    def stage(d, source, target):
        for at, part in pick(d, source):
            target[d, :, at] = part

    stage(order[0], rbuf, rsend)
    pl.semaphore_wait(barrier, n_dp + n_group - 2)

    def remote(src, dst, send, recv, who):
        return pltpu.make_async_remote_copy(
            src_ref=src, dst_ref=dst, send_sem=send, recv_sem=recv,
            device_id=who, device_id_type=MESH,
        )

    sent = []
    second = []
    for d, later in zip(order, order[1:] + [0]):
        stage(later, rbuf, rsend)
        k = dp_peer(d)
        sent.append(remote(rsend.at[d], out_r.at[me], rs_sem.at[d], rr_sem.at[d], (k, mine)))
        sent[-1].start()
    own = [pltpu.make_async_copy(rsend.at[0], out_r.at[me], own_sem.at[0])]
    own[0].start()

    for b in range(blocks):
        at = pl.ds(b * LANES, LANES)
        rate = jnp.transpose(jnp.broadcast_to(rate_ref[b : b + 1, :], (LANES, LANES)))
        length = jnp.transpose(jnp.broadcast_to(row_of(0, b), (LANES, LANES)))
        lenb[at, :] = length.astype(jnp.int32)
        bstep[at, :] = jnp.exp(-rate * wide)
        carry[at, :] = jnp.zeros((LANES, LANES), F32)
        for x in range(4):
            acc[x, at, :] = jnp.zeros((LANES, LANES), F32)
        for h in range(wide // LANES):
            offset = (lax.broadcasted_iota(jnp.int32, (LANES, LANES), 1) + h * LANES).astype(F32)
            lower[at, h * LANES : (h + 1) * LANES] = jnp.exp(-rate * offset)
            upper[at, h * LANES : (h + 1) * LANES] = jnp.exp(rate * offset)
    tri[...] = (
        lax.broadcasted_iota(jnp.int32, (wide, wide), 0)
        >= lax.broadcasted_iota(jnp.int32, (wide, wide), 1)
    ).astype(F32).astype(BF16)
    for load in loads:
        load.wait()

    reps = wide // LANES

    def column_step(i, _):
        col = pl.multiple_of((span // wide - 1 - i) * wide, wide)
        for b in range(blocks):
            at = pl.ds(b * LANES, LANES)
            length = lenb[at, :]
            position = col + lax.broadcasted_iota(jnp.int32, (LANES, wide), 1)
            valid = position < jnp.concatenate([length] * reps, axis=1)
            r = jnp.where(valid, rbuf[at, pl.ds(col, wide)].astype(F32), 0.0)
            s = r * lower[at, :]
            high = s.astype(BF16)
            low = (s - high.astype(F32)).astype(BF16)
            both = jnp.dot(
                jnp.concatenate([high, low], axis=0), tri[...], preferred_element_type=F32
            )
            c = carry[at, :]
            summed = both[:LANES] + both[LANES:] + jnp.concatenate([c] * reps, axis=1)
            carry[at, :] = bstep[at, :] * jnp.broadcast_to(summed[:, :1], (LANES, LANES))
            a = upper[at, :] * summed - vbuf[at, pl.ds(col, wide)].astype(F32)
            a = jnp.where(valid, a, 0.0).astype(BF16)
            abuf[at, pl.ds(col, wide)] = a
            a = a.astype(F32)
            for x, term in enumerate((r, a, r * r, a * a)):
                acc[x, at, :] += sum(term[:, h * LANES : (h + 1) * LANES] for h in range(reps))
        return 0

    lax.fori_loop(0, span // wide, column_step, 0)

    lane = lax.broadcasted_iota(jnp.int32, (LANES, LANES), 1)
    for b in range(blocks):
        at = pl.ds(b * LANES, LANES)
        terms = jnp.where(lane == 0, lenb[at, :].astype(F32), 0.0)
        for x in range(4):
            total = jnp.sum(acc[x, at, :], axis=1, keepdims=True)
            terms = jnp.where(lane == x + 1, total, terms)
        tbuf[at, :] = terms
    tstage[...] = jnp.zeros_like(tstage)

    def stage_second(d, _):
        stage(d, abuf, asend)
        for at, part in pick(d, tbuf):
            tstage[0:piece, :] = part
        tsend[d] = jnp.transpose(tstage[...])[0:8, :]
        return 0

    lax.fori_loop(0, n_dp, stage_second, 0)

    terms_sent = []
    for d in order:
        k = dp_peer(d)
        terms_sent.append(remote(tsend.at[d], trecv.at[me], ts_sem.at[d], tr_sem.at[d], (k, mine)))
        terms_sent[-1].start()
    trecv[me] = tsend[0]

    def send_second(part):
        at = pl.ds(*cuts[part])
        second.append([])
        for d in order:
            k = dp_peer(d)
            second[part].append(
                remote(
                    asend.at[d, :, at], out_a.at[me, :, at],
                    as_sem.at[part, d], ar_sem.at[part, d], (k, mine),
                )
            )
            second[part][-1].start()

    send_second(0)
    own.append(pltpu.make_async_copy(asend.at[0], out_a.at[me], own_sem.at[1]))
    own[1].start()

    for copy in terms_sent:
        copy.wait()

    row = lax.broadcasted_iota(jnp.int32, (LANES, LANES), 0).astype(F32)
    partial = jnp.zeros((8, LANES), F32)
    per_block = LANES // piece
    for b in range(blocks):
        picked = (row == row_of(1, b)).astype(F32)
        member = (row == row_of(2, b)).astype(F32)
        arrived_member = lax.dot_general(
            member.astype(BF16), picked.astype(BF16), NT, preferred_element_type=F32
        )
        terms = trecv[b * per_block]
        for s in range(1, per_block):
            terms = terms + pltpu.roll(trecv[b * per_block + s], s * piece, 1)
        partial = partial + lax.dot_general(
            terms, arrived_member, NT, precision=HIGHEST, preferred_element_type=F32
        )
        out_ch[b] = jnp.transpose(picked).astype(BF16)
        tot[b] = jnp.dot(terms, picked, precision=HIGHEST, preferred_element_type=F32)
    psend[...] = partial
    precv[me] = partial
    sums_sent = []
    for d in order:
        k = dp_peer(d)
        sums_sent.append(remote(psend, precv.at[me], ps_sem.at[d], pr_sem.at[d], (k, mine)))
        sums_sent[-1].start()

    for part in range(1, len(cuts)):
        send_second(part)

    for copy in sums_sent:
        copy.wait()
    partial = precv[0]
    for k in range(1, n_dp):
        partial = partial + precv[k]
    qsend[...] = partial
    qrecv[mine] = partial
    group_sent = []
    for d in range(1, n_group):
        k = group_peer(d)
        group_sent.append(remote(qsend, qrecv.at[mine], qs_sem.at[d], qr_sem.at[d], (me, k)))
        group_sent[-1].start()
    for copy in group_sent:
        copy.wait()
    total = qrecv[0]
    for k in range(1, n_group):
        total = total + qrecv[k]

    count = jnp.maximum(total[0:1, :], 1.0)
    means = total[1:3, :] / count
    spreads = jnp.maximum(total[3:5, :] / count - means * means, 0.0)
    scales = lax.rsqrt(spreads + 1e-05)
    table = jnp.concatenate([means, scales, jnp.zeros((4, LANES), F32)], axis=0)
    for b in range(blocks):
        at = pl.ds(b * LANES, LANES)
        member = (row == row_of(2, b)).astype(F32)
        here = jnp.dot(table, member, precision=HIGHEST, preferred_element_type=F32)
        here = jnp.concatenate(
            [here[0:4, :], tot[b, 0:1, :], jnp.zeros((LANES - 5, LANES), F32)], axis=0
        )
        out_st[at, :] = jnp.transpose(here)

    def whiten_part(x, source, target, start, width):
        tile = min(512, width)

        def tile_step(i, _):
            col = pl.multiple_of(start + i * tile, tile)
            for b in range(blocks):
                at = pl.ds(b * LANES, LANES)
                stats = out_st[at, :]
                position = (col + lax.broadcasted_iota(jnp.int32, (LANES, tile), 1)).astype(F32)
                arrived = source[b * per_block : (b + 1) * per_block, :, pl.ds(col, tile)]
                moved = jnp.dot(
                    out_ch[b], arrived.reshape(LANES, tile), preferred_element_type=F32
                )
                white = (moved - stats[:, x : x + 1]) * stats[:, x + 2 : x + 3]
                white = jnp.where(position < stats[:, 4:5], white, 0.0)
                target[at, pl.ds(col, tile)] = white.astype(BF16)
            return 0

        lax.fori_loop(0, width // tile, tile_step, 0)

    for copy in own + sent:
        copy.wait()
    whiten_part(0, out_r, white_r, 0, span)
    for part, copies in enumerate(second):
        for copy in copies:
            copy.wait_recv()
        whiten_part(1, out_a, white_a, *cuts[part])
    for copies in second:
        for copy in copies:
            copy.wait_send()


def exchange(n_dp, n_group, rewards, values, lengths, decay_rate, piece_dest, row_perm, minibatch):
    rows, span = rewards.shape
    blocks, block = row_perm.shape
    piece = rows // n_dp
    wide = 256
    vmem = pl.BlockSpec(memory_space=pltpu.VMEM)
    far = pl.BlockSpec(memory_space=pltpu.HBM)
    dma = pltpu.SemaphoreType.DMA
    whole = pltpu.VMEM((rows, span), BF16)
    staged = pltpu.VMEM((n_dp, piece, span), BF16)
    factor = pltpu.VMEM((rows, wide), F32)
    column = pltpu.VMEM((rows, LANES), F32)
    small = pltpu.VMEM((n_dp, 8, LANES), F32)
    one = pltpu.VMEM((8, LANES), F32)
    return pl.pallas_call(
        functools.partial(exchange_kernel, n_dp, n_group),
        out_shape=(jax.ShapeDtypeStruct((rows, span), BF16),) * 2,
        in_specs=[vmem, far, vmem, vmem],
        out_specs=(vmem, vmem),
        scratch_shapes=[
            staged, staged, column, pltpu.VMEM((blocks, LANES, LANES), BF16),
            whole, whole, staged, staged,
            pltpu.VMEM((wide, wide), BF16), factor, factor,
            pltpu.VMEM((rows, LANES), jnp.int32), column, column,
            pltpu.VMEM((4, rows, LANES), F32), column, pltpu.VMEM((LANES, LANES), F32),
            small, small, one, small, one, pltpu.VMEM((n_group, 8, LANES), F32),
            pltpu.VMEM((blocks, 8, LANES), F32),
            dma((4,)), dma((2,)), dma((n_dp,)), dma((n_dp,)), dma((3, n_dp)), dma((3, n_dp)),
            dma((n_dp,)), dma((n_dp,)), dma((n_dp,)), dma((n_dp,)), dma((n_group,)), dma((n_group,)),
        ],
        compiler_params=pltpu.CompilerParams(
            collective_id=0, has_side_effects=True, vmem_limit_bytes=50_000_000
        ),
    )(
        rewards, values, decay_rate.reshape(blocks, block),
        jnp.concatenate(
            [
                lengths.reshape(blocks, block),
                row_perm,
                minibatch.reshape(blocks, block),
                jnp.pad(piece_dest, ((0, 0), (0, block - piece_dest.shape[1]))),
            ],
            axis=0,
        ),
    )


def local(n_dp, n_group, rewards, values, lengths, decay_rate, piece_dest, row_perm, minibatch):
    rows, span = rewards.shape
    if (rows // n_dp) % 16 or LANES % (rows // n_dp) or row_perm.shape[1] != LANES or span % 4096:
        return plain_local(rewards, values, lengths, decay_rate, piece_dest, row_perm, minibatch)
    return exchange(
        n_dp, n_group, rewards, values, lengths, decay_rate, piece_dest, row_perm, minibatch
    )


def solution(mesh):
    return jax.shard_map(
        functools.partial(local, mesh.shape["dp"], mesh.shape["group"]),
        mesh=mesh,
        in_specs=(
            P(("dp", "group"), None),
            P(("dp", "group"), None),
            P(("dp", "group")),
            P(("dp", "group")),
            P("dp", None),
            P(("dp", "group"), None),
            P(("dp", "group")),
        ),
        out_specs=(P(("dp", "group"), None), P(("dp", "group"), None)),
        check_vma=False,
    )
```

profile of v0, /device:TPU:0, one launch (start us, length us, event | category | flops | bytes accessed | tf_op | source)
XLA Modules:
  0.0 105.9 jit_solution(4902204527948568095)
XLA Ops:
  0.6 0.7 pad_add_fusion.packed
  1.4 0.0 copy-start
  1.4 1.6 %copy-done = bf16[256,4096]{1,0:T(8,128)(2,1)S(1)} copy-done((bf16[256,4096]{1,0:T(8,128)(2,1)S(1)}, bf16[256,4096]{1,0:T(8,128)(2,1)}, u32[]{:S(2)}) %copy-start) | copy-done | bytes 2097176
  3.0 0.0 copy-start.1
  3.0 0.7 copy-done.1
  3.6 99.6 %shard_map.86 = (bf16[256,4096]{1,0:T(8,128)(2,1)S(1)}, bf16[256,4096]{1,0:T(8,128)(2,1)S(1)}) custom-call(bf16[256,4096]{1,0:T(8,128)(2,1)S(1)} %copy-done, bf16[256,4096]{1,0:T(8,128)(2,1)} %val_hbm.1, f32[2,128]{1,0:T(2,128)S(1)} %bitcast.3, s32[7,128]{1,0:T(8,128)S(1)} %pad_add_fusion.packed), custom_call_target="tpu_custom_call" | custom-call | tf_op jit(solution)/shard_map/pallas_call | solution.py:416
  103.3 1.3 %copy.11 = bf16[256,4096]{1,0:T(8,128)(2,1)} copy(bf16[256,4096]{1,0:T(8,128)(2,1)S(1)} %get-tuple-element.4) | data formatting | bytes 4194304
  104.6 1.3 %copy.12 = bf16[256,4096]{1,0:T(8,128)(2,1)} copy(bf16[256,4096]{1,0:T(8,128)(2,1)S(1)} %get-tuple-element.5) | data formatting | bytes 4194304
Async XLA Ops:
  1.4 1.6 %copy-start = (bf16[256,4096]{1,0:T(8,128)(2,1)S(1)}, bf16[256,4096]{1,0:T(8,128)(2,1)}, u32[]{:S(2)}) copy-start(bf16[256,4096]{1,0:T(8,128)(2,1)} %rbuf.1) | copy-start | bytes 6291460
  3.0 0.7 copy-start.1
where the time goes:
time: 106 us
  Pallas kernels  99.6 us (94%)
  local copies, waits for them, and re-layouts  4.91 us (5%)
    pallas_call x1, Pallas kernels, exchange(): pl.pallas_call(functools.partial(exchange_kernel, n_dp, n_group), out_sha...  99.6 us
    unnamed x6, local copies, waits for them, and re-layouts  4.91 us

commit v1 on v0

--- a/solution.py
+++ b/solution.py
@@ -430,7 +430,7 @@
             dma((n_dp,)), dma((n_dp,)), dma((n_dp,)), dma((n_dp,)), dma((n_group,)), dma((n_group,)),
         ],
         compiler_params=pltpu.CompilerParams(
-            collective_id=0, has_side_effects=True, vmem_limit_bytes=50_000_000
+            collective_id=1, has_side_effects=True, vmem_limit_bytes=50_000_000
         ),
     )(
         rewards, values, decay_rate.reshape(blocks, block),
@@ -446,12 +446,477 @@
     )
 
 
+def ragged_kernel(
+    n_dp, n_group, cap,
+    rew_hbm, val_hbm, len_hbm, rate_hbm, dest_hbm, perm_hbm, mini_hbm,
+    white_r, white_a, over_out,
+    rbuf, vbuf, abuf, len_v, rate_v, perm_v, mini_v, dest_v,
+    dsend, psend, dense, packed, chooser, placer, spread,
+    out_st, out_ch, tri, lower, upper, lenb, bstep, carry,
+    acc, tbuf, tstage, tsend, trecv, psum, precv, qsum, qrecv, tot,
+    load_sem, meta_sem, own_sem, ds_sem, dr_sem, ks_sem, kr_sem,
+    ts_sem, tr_sem, ps_sem, pr_sem, qs_sem, qr_sem,
+):
+    rows, span = rbuf.shape
+    blocks = out_ch.shape[0]
+    piece = rows // n_dp
+    half = n_dp // 2
+    chunks = span // LANES
+    depth = placer.shape[2]
+    wide = tri.shape[0]
+    cuts = part_cuts(cap)
+    me = lax.axis_index("dp")
+    mine = lax.axis_index("group")
+    side = me // half
+    spot = lax.rem(me, half)
+
+    def dp_peer(d):
+        return lax.rem(me + d, n_dp)
+
+    def group_peer(d):
+        return lax.rem(mine + d, n_group)
+
+    def near(j):
+        return side * half + lax.rem(me + j, half)
+
+    def across(j):
+        return (1 - side) * half + lax.rem(me + j, half)
+
+    small = []
+    for i, (src, dst) in enumerate(
+        ((len_hbm, len_v), (dest_hbm, dest_v), (rate_hbm, rate_v), (perm_hbm, perm_v), (mini_hbm, mini_v))
+    ):
+        small.append(pltpu.make_async_copy(src, dst, meta_sem.at[i]))
+        small[-1].start()
+    quarter = rows // 4
+    loads = []
+    for x, (src, dst) in enumerate(((rew_hbm, rbuf), (val_hbm, vbuf))):
+        for part in range(4):
+            at = pl.ds(part * quarter, quarter)
+            loads.append(pltpu.make_async_copy(src.at[at], dst.at[at], load_sem.at[x, part]))
+            loads[-1].start()
+
+    barrier = pltpu.get_barrier_semaphore()
+    for d in range(1, n_dp):
+        pl.semaphore_signal(barrier, inc=1, device_id=(dp_peer(d), mine), device_id_type=MESH)
+    for d in range(1, n_group):
+        pl.semaphore_signal(barrier, inc=1, device_id=(me, group_peer(d)), device_id_type=MESH)
+
+    lane = lax.broadcasted_iota(jnp.int32, (LANES, LANES), 1)
+    sub = lax.broadcasted_iota(jnp.int32, (LANES, LANES), 0)
+    before = jnp.logical_and(sub // piece == lane // piece, sub < lane).astype(F32).astype(BF16)
+    per_vreg = LANES // piece
+
+    def used(length):
+        return ((length + (LANES - 1)) // LANES).astype(F32).astype(BF16)
+
+    for copy in small:
+        copy.wait()
+
+    dests = [dest_v[0:1, p : p + 1] for p in range(n_dp)]
+    targets = [jnp.broadcast_to(dest.astype(F32), (piece, LANES)) for dest in dests]
+    row_dest = []
+    for b in range(blocks):
+        here = jnp.zeros((16, LANES), jnp.int32)
+        for q in range(per_vreg):
+            here = jnp.where(lane[0:16] // piece == q, dests[b * per_vreg + q], here)
+        row_dest.append(here)
+    fold = (sub % piece == lane % piece).astype(F32).astype(BF16)
+
+    def pick(k, source):
+        k = jnp.full((piece, LANES), k, jnp.int32).astype(F32)
+        weights = [(target == k).astype(F32).astype(source.dtype) for target in targets]
+        for c in range(0, source.shape[1], LANES):
+            at = slice(c, c + LANES)
+            yield at, sum(source[p * piece : (p + 1) * piece, at] * weights[p] for p in range(n_dp))
+
+    def choose(j, over):
+        wanted = jnp.zeros((16, LANES), F32)
+        for b in range(blocks):
+            here = jnp.broadcast_to(len_v[b : b + 1, :], (16, LANES))
+            here = jnp.where(row_dest[b] == across(j), here, 0)
+            wanted = wanted + jnp.dot(used(here), fold, preferred_element_type=F32)
+        base = jnp.dot(wanted.astype(BF16), before, preferred_element_type=F32)
+        over = jnp.maximum(over, jnp.where(base + wanted > cap, 1.0, 0.0)[0:8])
+        base = base.astype(jnp.int32)[0:1]
+        wanted = wanted.astype(jnp.int32)[0:1]
+        place = lax.broadcasted_iota(jnp.int32, (cap, LANES), 0)
+        for v in range(chunks // per_vreg):
+            c = lane[0:1] // piece + v * per_vreg
+            key = jnp.where(c < wanted, base + c, -1)
+            chooser[j, :, v * LANES : (v + 1) * LANES] = (place == key).astype(F32).astype(BF16)
+        return over
+
+    over = lax.fori_loop(0, half, choose, jnp.zeros((8, LANES), F32))
+
+    def pack(x, j, source):
+        arranged = jnp.concatenate([part for _, part in pick(across(j), source)], axis=0)
+        psend[x, j] = jnp.dot(chooser[j], arranged, preferred_element_type=F32).astype(BF16)
+
+    def copy_dense(x, j, source):
+        for at, part in pick(near(j), source):
+            dsend[x, j, :, at] = part
+
+    packed_tail = packed.shape[2] - cap
+    if packed_tail:
+        packed[:, :, cap:, :] = jnp.zeros((2, half, packed_tail, LANES), BF16)
+
+    for load in loads[:4]:
+        load.wait()
+
+    def remote(src, dst, send, recv, who):
+        return pltpu.make_async_remote_copy(
+            src_ref=src, dst_ref=dst, send_sem=send, recv_sem=recv,
+            device_id=who, device_id_type=MESH,
+        )
+
+    def dense_copy(x, j):
+        return remote(
+            dsend.at[x, j], dense.at[x, spot], ds_sem.at[x, j], dr_sem.at[x, j], (near(j), mine)
+        )
+
+    def packed_copy(x, j, part):
+        at = pl.ds(*cuts[x][part])
+        return remote(
+            psend.at[x, j, at], packed.at[x, spot, at],
+            ks_sem.at[x, part, j], kr_sem.at[x, part, j], (across(j), mine),
+        )
+
+    order = []
+    for j in range(half):
+        order.append((0, j))
+        if j + 1 < half:
+            order.append((1, j + 1))
+
+    def stage(item):
+        kind, j = item
+        (copy_dense if kind else pack)(0, j, rbuf)
+
+    def issue(x, item):
+        kind, j = item
+        copy = dense_copy(x, j) if kind else packed_copy(x, j, 0)
+        copy.start()
+        return copy
+
+    dense_sent = [[], []]
+    packed_sent = [[[]], [[] for _ in cuts[1]]]
+    stage(order[0])
+    pl.semaphore_wait(barrier, n_dp + n_group - 2)
+    for item, later in zip(order, order[1:] + [(1, 0)]):
+        stage(later)
+        (dense_sent[0] if item[0] else packed_sent[0][0]).append(issue(0, item))
+    own = [pltpu.make_async_copy(dsend.at[0, 0], dense.at[0, spot], own_sem.at[0])]
+    own[0].start()
+
+    for b in range(blocks):
+        at = pl.ds(b * LANES, LANES)
+        rate = jnp.transpose(jnp.broadcast_to(rate_v[b : b + 1, :], (LANES, LANES)))
+        length = jnp.transpose(jnp.broadcast_to(len_v[b : b + 1, :].astype(F32), (LANES, LANES)))
+        lenb[at, :] = length.astype(jnp.int32)
+        bstep[at, :] = jnp.exp(-rate * wide)
+        carry[at, :] = jnp.zeros((LANES, LANES), F32)
+        for x in range(4):
+            acc[x, at, :] = jnp.zeros((LANES, LANES), F32)
+        for i in range(wide // LANES):
+            offset = (lane + i * LANES).astype(F32)
+            lower[at, i * LANES : (i + 1) * LANES] = jnp.exp(-rate * offset)
+            upper[at, i * LANES : (i + 1) * LANES] = jnp.exp(rate * offset)
+    tri[...] = (
+        lax.broadcasted_iota(jnp.int32, (wide, wide), 0)
+        >= lax.broadcasted_iota(jnp.int32, (wide, wide), 1)
+    ).astype(F32).astype(BF16)
+    for load in loads[4:]:
+        load.wait()
+
+    reps = wide // LANES
+
+    def column_step(i, _):
+        col = pl.multiple_of((span // wide - 1 - i) * wide, wide)
+        for b in range(blocks):
+            at = pl.ds(b * LANES, LANES)
+            length = lenb[at, :]
+            position = col + lax.broadcasted_iota(jnp.int32, (LANES, wide), 1)
+            valid = position < jnp.concatenate([length] * reps, axis=1)
+            r = jnp.where(valid, rbuf[at, pl.ds(col, wide)].astype(F32), 0.0)
+            s = r * lower[at, :]
+            high = s.astype(BF16)
+            low = (s - high.astype(F32)).astype(BF16)
+            both = jnp.dot(
+                jnp.concatenate([high, low], axis=0), tri[...], preferred_element_type=F32
+            )
+            c = carry[at, :]
+            summed = both[:LANES] + both[LANES:] + jnp.concatenate([c] * reps, axis=1)
+            carry[at, :] = bstep[at, :] * jnp.broadcast_to(summed[:, :1], (LANES, LANES))
+            a = upper[at, :] * summed - vbuf[at, pl.ds(col, wide)].astype(F32)
+            a = jnp.where(valid, a, 0.0).astype(BF16)
+            abuf[at, pl.ds(col, wide)] = a
+            a = a.astype(F32)
+            for x, term in enumerate((r, a, r * r, a * a)):
+                acc[x, at, :] += sum(term[:, i * LANES : (i + 1) * LANES] for i in range(reps))
+        return 0
+
+    lax.fori_loop(0, span // wide, column_step, 0)
+
+    for b in range(blocks):
+        at = pl.ds(b * LANES, LANES)
+        terms = jnp.where(lane == 0, lenb[at, :].astype(F32), 0.0)
+        for x in range(4):
+            total = jnp.sum(acc[x, at, :], axis=1, keepdims=True)
+            terms = jnp.where(lane == x + 1, total, terms)
+        tbuf[at, :] = terms
+    tstage[...] = jnp.zeros_like(tstage)
+
+    def stage_terms(d, _):
+        for at, part in pick(dp_peer(d), tbuf):
+            tstage[0:piece, :] = part
+        tsend[d] = jnp.transpose(tstage[...])[0:8, :]
+        return 0
+
+    lax.fori_loop(0, n_dp, stage_terms, 0)
+
+    def stage_second(j, _):
+        copy_dense(1, j, abuf)
+        pack(1, j, abuf)
+        return 0
+
+    lax.fori_loop(0, half, stage_second, 0)
+
+    terms_sent = []
+    for d in range(1, n_dp):
+        k = dp_peer(d)
+        terms_sent.append(remote(tsend.at[d], trecv.at[me], ts_sem.at[d], tr_sem.at[d], (k, mine)))
+        terms_sent[-1].start()
+    trecv[me] = tsend[0]
+
+    for item in order:
+        (dense_sent[1] if item[0] else packed_sent[1][0]).append(issue(1, item))
+    own.append(pltpu.make_async_copy(dsend.at[1, 0], dense.at[1, spot], own_sem.at[1]))
+    own[1].start()
+
+    for copy in terms_sent:
+        copy.wait()
+
+    row = sub.astype(F32)
+    partial = jnp.where(lax.broadcasted_iota(jnp.int32, (8, LANES), 0) == 5, over, 0.0)
+    per_block = LANES // piece
+    for b in range(blocks):
+        picked = (row == perm_v[b : b + 1, :].astype(F32)).astype(F32)
+        member = (row == mini_v[b : b + 1, :].astype(F32)).astype(F32)
+        arrived_member = lax.dot_general(
+            member.astype(BF16), picked.astype(BF16), NT, preferred_element_type=F32
+        )
+        terms = trecv[b * per_block]
+        for s in range(1, per_block):
+            terms = terms + pltpu.roll(trecv[b * per_block + s], s * piece, 1)
+        partial = partial + lax.dot_general(
+            terms, arrived_member, NT, precision=HIGHEST, preferred_element_type=F32
+        )
+        out_ch[b] = jnp.transpose(picked).astype(BF16)
+        tot[b] = jnp.dot(terms, picked, precision=HIGHEST, preferred_element_type=F32)
+    psum[...] = partial
+    precv[me] = partial
+    sums_sent = []
+    for d in range(1, n_dp):
+        k = dp_peer(d)
+        sums_sent.append(remote(psum, precv.at[me], ps_sem.at[d], pr_sem.at[d], (k, mine)))
+        sums_sent[-1].start()
+
+    for part in range(1, len(cuts[1])):
+        for j in range(half):
+            packed_sent[1][part].append(packed_copy(1, j, part))
+            packed_sent[1][part][-1].start()
+
+    other = 1 - side
+    length = trecv[other * per_block]
+    for s in range(1, per_block):
+        length = length + pltpu.roll(trecv[other * per_block + s], s * piece, 1)
+    length = jnp.broadcast_to(length[0:1], (16, LANES)).astype(jnp.int32)
+    wanted = used(length)
+    base = jnp.dot(wanted, before, preferred_element_type=F32)
+    base = jnp.transpose(jnp.broadcast_to(base[0:1], (LANES, LANES))).astype(jnp.int32)
+    wanted = jnp.transpose(jnp.broadcast_to(wanted.astype(F32)[0:1], (LANES, LANES))).astype(jnp.int32)
+
+    def place_chunk(c, _):
+        key = jnp.where(c < wanted, base + c, -1)
+        at = pl.ds(pl.multiple_of(c * piece, piece), piece)
+        for n in range(depth // LANES):
+            match = (lane + n * LANES == key).astype(F32).astype(BF16)
+            for q in range(half):
+                placer[q, at, n * LANES : (n + 1) * LANES] = match[q * piece : (q + 1) * piece]
+        return 0
+
+    lax.fori_loop(0, chunks, place_chunk, 0)
+
+    def unpack(x, start, stop, first):
+        stop = depth if stop == cap else stop
+
+        def one(q, _):
+            got = jnp.dot(
+                placer[q, :, start:stop], packed[x, q, start:stop, :], preferred_element_type=F32
+            ).astype(BF16)
+            at = pl.ds(pl.multiple_of(q * piece, piece), piece)
+            for c in range(chunks):
+                cols = slice(c * LANES, (c + 1) * LANES)
+                part = got[c * piece : (c + 1) * piece]
+                spread[x, at, cols] = part if first else spread[x, at, cols] + part
+            return 0
+
+        lax.fori_loop(0, half, one, 0)
+
+    for copy in own[:1] + dense_sent[0] + packed_sent[0][0]:
+        copy.wait()
+    unpack(0, 0, cap, True)
+
+    for copy in sums_sent:
+        copy.wait()
+    partial = precv[0]
+    for k in range(1, n_dp):
+        partial = partial + precv[k]
+    qsum[...] = partial
+    qrecv[mine] = partial
+    group_sent = []
+    for d in range(1, n_group):
+        k = group_peer(d)
+        group_sent.append(remote(qsum, qrecv.at[mine], qs_sem.at[d], qr_sem.at[d], (me, k)))
+        group_sent[-1].start()
+    for copy in group_sent:
+        copy.wait()
+    total = qrecv[0]
+    for k in range(1, n_group):
+        total = total + qrecv[k]
+    over_out[0] = jnp.max(total[5:6, :])
+
+    count = jnp.maximum(total[0:1, :], 1.0)
+    means = total[1:3, :] / count
+    spreads = jnp.maximum(total[3:5, :] / count - means * means, 0.0)
+    scales = lax.rsqrt(spreads + 1e-05)
+    table = jnp.concatenate([means, scales, jnp.zeros((4, LANES), F32)], axis=0)
+    for b in range(blocks):
+        at = pl.ds(b * LANES, LANES)
+        member = (row == mini_v[b : b + 1, :].astype(F32)).astype(F32)
+        here = jnp.dot(table, member, precision=HIGHEST, preferred_element_type=F32)
+        here = jnp.concatenate(
+            [here[0:4, :], tot[b, 0:1, :], jnp.zeros((LANES - 5, LANES), F32)], axis=0
+        )
+        out_st[at, :] = jnp.transpose(here)
+
+    def whiten_block(x, arrived_at, b, target):
+        tile = 512
+
+        def tile_step(i, _):
+            col = pl.multiple_of(i * tile, tile)
+            at = pl.ds(pl.multiple_of(b * LANES, LANES), LANES)
+            stats = out_st[at, :]
+            position = (col + lax.broadcasted_iota(jnp.int32, (LANES, tile), 1)).astype(F32)
+            moved = jnp.dot(out_ch[b], arrived_at(pl.ds(col, tile)), preferred_element_type=F32)
+            white = (moved - stats[:, x : x + 1]) * stats[:, x + 2 : x + 3]
+            white = jnp.where(position < stats[:, 4:5], white, 0.0)
+            target[at, pl.ds(col, tile)] = white.astype(BF16)
+            return 0
+
+        lax.fori_loop(0, span // tile, tile_step, 0)
+
+    def whiten_dense(x, target):
+        whiten_block(x, lambda at: dense[x, :, :, at].reshape(LANES, at.size), side, target)
+
+    def whiten_packed(x, target):
+        whiten_block(x, lambda at: spread[x, :, at], other, target)
+
+    whiten_dense(0, white_r)
+    whiten_packed(0, white_r)
+    for copy in own[1:] + dense_sent[1]:
+        copy.wait()
+    whiten_dense(1, white_a)
+    for part, copies in enumerate(packed_sent[1]):
+        for copy in copies:
+            copy.wait_recv()
+        start, size = cuts[1][part]
+        unpack(1, start, start + size, part == 0)
+    whiten_packed(1, white_a)
+    for copies in packed_sent[1]:
+        for copy in copies:
+            copy.wait_send()
+
+
+def part_cuts(cap):
+    a, b = cap // 256 * 128, cap // 128 * 128
+    b = b - 128 if cap - b < 64 else b
+    return (((0, cap),), ((0, a), (a, b - a), (b, cap - b)))
+
+
+def ragged_capacity(rows, n_dp, span):
+    chunks = rows // n_dp * (span // LANES)
+    return chunks * 23 // 32 // 16 * 16
+
+
+def ragged(n_dp, n_group, rewards, values, lengths, decay_rate, piece_dest, row_perm, minibatch):
+    rows, span = rewards.shape
+    blocks, block = row_perm.shape
+    piece = rows // n_dp
+    half = n_dp // 2
+    wide = 256
+    cap = ragged_capacity(rows, n_dp, span)
+    depth = -(-cap // LANES) * LANES
+    chunks = piece * (span // LANES)
+    vmem = pl.BlockSpec(memory_space=pltpu.VMEM)
+    far = pl.BlockSpec(memory_space=pltpu.HBM)
+    dma = pltpu.SemaphoreType.DMA
+    whole = pltpu.VMEM((rows, span), BF16)
+    factor = pltpu.VMEM((rows, wide), F32)
+    column = pltpu.VMEM((rows, LANES), F32)
+    small = pltpu.VMEM((n_dp, 8, LANES), F32)
+    one = pltpu.VMEM((8, LANES), F32)
+    meta = pltpu.VMEM((blocks, LANES), jnp.int32)
+    dense = pltpu.VMEM((2, half, piece, span), BF16)
+    parts = len(part_cuts(cap)[1])
+    return pl.pallas_call(
+        functools.partial(ragged_kernel, n_dp, n_group, cap),
+        out_shape=(jax.ShapeDtypeStruct((rows, span), BF16),) * 2
+        + (jax.ShapeDtypeStruct((1,), F32),),
+        in_specs=[far] * 7,
+        out_specs=(vmem, vmem, pl.BlockSpec(memory_space=pltpu.SMEM)),
+        scratch_shapes=[
+            whole, whole, whole, meta, pltpu.VMEM((blocks, LANES), F32), meta, meta,
+            pltpu.VMEM((1, n_dp), jnp.int32),
+            dense, pltpu.VMEM((2, half, cap, LANES), BF16),
+            dense, pltpu.VMEM((2, half, depth, LANES), BF16),
+            pltpu.VMEM((half, cap, chunks), BF16), pltpu.VMEM((half, chunks, depth), BF16),
+            pltpu.VMEM((2, LANES, span), BF16),
+            column, pltpu.VMEM((blocks, LANES, LANES), BF16),
+            pltpu.VMEM((wide, wide), BF16), factor, factor,
+            pltpu.VMEM((rows, LANES), jnp.int32), column, column,
+            pltpu.VMEM((4, rows, LANES), F32), column, pltpu.VMEM((LANES, LANES), F32),
+            small, small, one, small, one, pltpu.VMEM((n_group, 8, LANES), F32),
+            pltpu.VMEM((blocks, 8, LANES), F32),
+            dma((2, 4)), dma((5,)), dma((2,)), dma((2, half)), dma((2, half)),
+            dma((2, parts, half)), dma((2, parts, half)),
+            dma((n_dp,)), dma((n_dp,)), dma((n_dp,)), dma((n_dp,)), dma((n_group,)), dma((n_group,)),
+        ],
+        compiler_params=pltpu.CompilerParams(
+            collective_id=0, has_side_effects=True, vmem_limit_bytes=60_000_000
+        ),
+    )(
+        rewards, values, lengths.reshape(blocks, block), decay_rate.reshape(blocks, block),
+        piece_dest, row_perm, minibatch.reshape(blocks, block),
+    )
+
+
 def local(n_dp, n_group, rewards, values, lengths, decay_rate, piece_dest, row_perm, minibatch):
     rows, span = rewards.shape
-    if (rows // n_dp) % 16 or LANES % (rows // n_dp) or row_perm.shape[1] != LANES or span % 4096:
-        return plain_local(rewards, values, lengths, decay_rate, piece_dest, row_perm, minibatch)
-    return exchange(
-        n_dp, n_group, rewards, values, lengths, decay_rate, piece_dest, row_perm, minibatch
+    blocks, block = row_perm.shape
+    piece = rows // n_dp
+    args = (rewards, values, lengths, decay_rate, piece_dest, row_perm, minibatch)
+    if piece % 16 or LANES % piece or block != LANES or span % 4096:
+        return plain_local(*args)
+    whole = functools.partial(exchange, n_dp, n_group)
+    if n_dp % 2 or blocks != 2 or n_dp // 2 * piece != LANES:
+        return whole(*args)
+    white_rewards, white_advantage, over = ragged(n_dp, n_group, *args)
+    return lax.cond(
+        over[0] > 0.0,
+        lambda kept, args: whole(*args),
+        lambda kept, args: kept,
+        (white_rewards, white_advantage), args,
     )
 
 

time: 106 us -> 92 us (0.87)
  Pallas kernels: 99.6 us -> 85.6 us
    pallas_call x1, Pallas kernels: 99.6 us -> 85.6 us  [ragged(): pl.pallas_call(functools.partial(ragged_kernel, n_dp, n_group, cap), out_...]
    unnamed x6 -> x16, local copies, waits for them, and re-layouts: 4.91 us -> 4.63 us
where the time goes in v1:
time: 92 us; the launch traced here: 91.9 us
  Pallas kernels  85.6 us (93%)
  local copies, waits for them, and re-layouts  4.63 us (5%)
  between operations  1.43 us (2%)
    pallas_call x1, Pallas kernels, ragged(): pl.pallas_call(functools.partial(ragged_kernel, n_dp, n_group, cap), out_...  85.6 us
    unnamed x16, local copies, waits for them, and re-layouts  4.63 us

profile of v1, /device:TPU:0, one launch (start us, length us, event | category | flops | bytes accessed | tf_op | source)
XLA Modules:
  0.0 91.9 jit_solution(18353733044825315470)
XLA Ops:
  0.6 0.0 copy-start
  0.6 0.0 copy-start.2
  0.7 0.0 copy-start.3
  0.7 0.0 copy-start.4
  0.7 0.0 copy-start.5
  0.7 0.0 copy-start.6
  0.7 85.6 %shard_map.90 = (bf16[256,4096]{1,0:T(8,128)(2,1)}, bf16[256,4096]{1,0:T(8,128)(2,1)}, f32[1]{0:T(128)}) custom-call(bf16[256,4096]{1,0:T(8,128)(2,1)} %rew_hbm.1, bf16[256,4096]{1,0:T(8,128)(2,1)} %val_hbm.1, s32[2,128]{1,0:T(2,128)} %bitcast.7, f32[2,128]{1,0:T(2,128)} %bitcast.11, s32[1,8]{1,0:T(1,128)} %dest_hbm.1, s32[2,128]{1,0:T(2,128)} %perm_hbm.1, ...), custom_call_target="tpu_custom_call" | custom-call | tf_op jit(solution)/shard_map/pallas_call | solution.py:872
  87.0 0.0 copy-done
  87.0 0.0 copy-done.2
  87.0 0.0 copy-done.3
  87.0 0.0 copy-done.4
  87.0 0.0 copy-done.5
  87.0 0.0 copy-done.6
  87.1 0.2 conditional.1
  87.2 0.0 copy-start.1
  87.3 3.3 %copy.19 = bf16[256,4096]{1,0:T(8,128)(2,1)} copy(bf16[256,4096]{1,0:T(8,128)(2,1)} %get-tuple-element.45) | data formatting | bytes 4194304
  90.5 0.0 copy-done.1
  90.5 1.3 %copy.20 = bf16[256,4096]{1,0:T(8,128)(2,1)} copy(bf16[256,4096]{1,0:T(8,128)(2,1)S(1)} %copy-done.1) | data formatting | bytes 4194304
Async XLA Ops:
  0.6 86.4 %copy-start = (bf16[256,4096]{1,0:T(8,128)(2,1)S(1)}, bf16[256,4096]{1,0:T(8,128)(2,1)}, u32[]{:S(2)}) copy-start(bf16[256,4096]{1,0:T(8,128)(2,1)} %rew_hbm.1) | copy-start | bytes 6291460
  0.6 86.4 %copy-start.2 = (s32[256]{0:T(256)S(1)}, s32[256]{0:T(256)}, u32[]{:S(2)}) copy-start(s32[256]{0:T(256)} %param.11) | copy-start | bytes 3076
  0.7 86.4 %copy-start.3 = (s32[2,128]{1,0:T(2,128)S(1)}, s32[2,128]{1,0:T(2,128)}, u32[]{:S(2)}) copy-start(s32[2,128]{1,0:T(2,128)} %perm_hbm.1) | copy-start | bytes 3076
  0.7 86.4 %copy-start.4 = (s32[256]{0:T(256)S(1)}, s32[256]{0:T(256)}, u32[]{:S(2)}) copy-start(s32[256]{0:T(256)} %param.15) | copy-start | bytes 3076
  0.7 86.4 %copy-start.5 = (f32[256]{0:T(256)S(1)}, f32[256]{0:T(256)}, u32[]{:S(2)}) copy-start(f32[256]{0:T(256)} %param.12) | copy-start | bytes 3076
  0.7 86.4 %copy-start.6 = (s32[1,8]{1,0:T(1,128)S(1)}, s32[1,8]{1,0:T(1,128)}, u32[]{:S(2)}) copy-start(s32[1,8]{1,0:T(1,128)} %dest_hbm.1) | copy-start | bytes 100
  87.2 3.3 %copy-start.1 = (bf16[256,4096]{1,0:T(8,128)(2,1)S(1)}, bf16[256,4096]{1,0:T(8,128)(2,1)}, u32[]{:S(2)}) copy-start(bf16[256,4096]{1,0:T(8,128)(2,1)} %get-tuple-element.46) | copy-start | bytes 6291460

commit v2 on v1

--- a/solution.py
+++ b/solution.py
@@ -430,7 +430,7 @@
             dma((n_dp,)), dma((n_dp,)), dma((n_dp,)), dma((n_dp,)), dma((n_group,)), dma((n_group,)),
         ],
         compiler_params=pltpu.CompilerParams(
-            collective_id=1, has_side_effects=True, vmem_limit_bytes=50_000_000
+            collective_id=1, has_side_effects=True, vmem_limit_bytes=36_000_000
         ),
     )(
         rewards, values, decay_rate.reshape(blocks, block),
@@ -449,8 +449,8 @@
 def ragged_kernel(
     n_dp, n_group, cap,
     rew_hbm, val_hbm, len_hbm, rate_hbm, dest_hbm, perm_hbm, mini_hbm,
-    white_r, white_a, over_out,
-    rbuf, vbuf, abuf, len_v, rate_v, perm_v, mini_v, dest_v,
+    white_far, white_a, over_out, unused_r, unused_a,
+    rbuf, vbuf, abuf, white_r, len_v, rate_v, perm_v, mini_v, dest_v,
     dsend, psend, dense, packed, chooser, placer, spread,
     out_st, out_ch, tri, lower, upper, lenb, bstep, carry,
     acc, tbuf, tstage, tsend, trecv, psum, precv, qsum, qrecv, tot,
@@ -547,8 +547,6 @@
             chooser[j, :, v * LANES : (v + 1) * LANES] = (place == key).astype(F32).astype(BF16)
         return over
 
-    over = lax.fori_loop(0, half, choose, jnp.zeros((8, LANES), F32))
-
     def pack(x, j, source):
         arranged = jnp.concatenate([part for _, part in pick(across(j), source)], axis=0)
         psend[x, j] = jnp.dot(chooser[j], arranged, preferred_element_type=F32).astype(BF16)
@@ -588,9 +586,15 @@
         if j + 1 < half:
             order.append((1, j + 1))
 
+    overs = [jnp.zeros((8, LANES), F32)]
+
     def stage(item):
         kind, j = item
-        (copy_dense if kind else pack)(0, j, rbuf)
+        if kind:
+            copy_dense(0, j, rbuf)
+        else:
+            overs.append(choose(j, overs[-1]))
+            pack(0, j, rbuf)
 
     def issue(x, item):
         kind, j = item
@@ -697,7 +701,7 @@
         copy.wait()
 
     row = sub.astype(F32)
-    partial = jnp.where(lax.broadcasted_iota(jnp.int32, (8, LANES), 0) == 5, over, 0.0)
+    partial = jnp.where(lax.broadcasted_iota(jnp.int32, (8, LANES), 0) == 5, overs[-1], 0.0)
     per_block = LANES // piece
     for b in range(blocks):
         picked = (row == perm_v[b : b + 1, :].astype(F32)).astype(F32)
@@ -824,6 +828,8 @@
 
     whiten_dense(0, white_r)
     whiten_packed(0, white_r)
+    kept = pltpu.make_async_copy(white_r, white_far, own_sem.at[2])
+    kept.start()
     for copy in own[1:] + dense_sent[1]:
         copy.wait()
     whiten_dense(1, white_a)
@@ -836,6 +842,7 @@
     for copies in packed_sent[1]:
         for copy in copies:
             copy.wait_send()
+    kept.wait()
 
 
 def part_cuts(cap):
@@ -872,11 +879,12 @@
     return pl.pallas_call(
         functools.partial(ragged_kernel, n_dp, n_group, cap),
         out_shape=(jax.ShapeDtypeStruct((rows, span), BF16),) * 2
-        + (jax.ShapeDtypeStruct((1,), F32),),
+        + (jax.ShapeDtypeStruct((1,), F32),)
+        + (jax.ShapeDtypeStruct((rows, span), BF16),) * 2,
         in_specs=[far] * 7,
-        out_specs=(vmem, vmem, pl.BlockSpec(memory_space=pltpu.SMEM)),
+        out_specs=(far, vmem, pl.BlockSpec(memory_space=pltpu.SMEM), far, far),
         scratch_shapes=[
-            whole, whole, whole, meta, pltpu.VMEM((blocks, LANES), F32), meta, meta,
+            whole, whole, whole, whole, meta, pltpu.VMEM((blocks, LANES), F32), meta, meta,
             pltpu.VMEM((1, n_dp), jnp.int32),
             dense, pltpu.VMEM((2, half, cap, LANES), BF16),
             dense, pltpu.VMEM((2, half, depth, LANES), BF16),
@@ -888,16 +896,71 @@
             pltpu.VMEM((4, rows, LANES), F32), column, pltpu.VMEM((LANES, LANES), F32),
             small, small, one, small, one, pltpu.VMEM((n_group, 8, LANES), F32),
             pltpu.VMEM((blocks, 8, LANES), F32),
-            dma((2, 4)), dma((5,)), dma((2,)), dma((2, half)), dma((2, half)),
+            dma((2, 4)), dma((5,)), dma((3,)), dma((2, half)), dma((2, half)),
             dma((2, parts, half)), dma((2, parts, half)),
             dma((n_dp,)), dma((n_dp,)), dma((n_dp,)), dma((n_dp,)), dma((n_group,)), dma((n_group,)),
         ],
         compiler_params=pltpu.CompilerParams(
-            collective_id=0, has_side_effects=True, vmem_limit_bytes=60_000_000
+            collective_id=0, has_side_effects=True, vmem_limit_bytes=44_000_000
         ),
     )(
         rewards, values, lengths.reshape(blocks, block), decay_rate.reshape(blocks, block),
         piece_dest, row_perm, minibatch.reshape(blocks, block),
+    )
+
+
+def write_kernel(over, from_r, from_a, whole_r, whole_a, to_r, to_a, bounce, sem):
+    quarter = from_r.shape[0] // 4
+
+    def move(sources, targets):
+        copies = []
+        for x, (src, dst) in enumerate(zip(sources, targets)):
+            for part in range(4):
+                at = pl.ds(part * quarter, quarter)
+                copies.append(pltpu.make_async_copy(src.at[at], dst.at[at], sem.at[x, part]))
+                copies[-1].start()
+        for copy in copies:
+            copy.wait()
+
+    @pl.when(over[0] > 0.0)
+    def _():
+        for source, target in ((whole_r, to_r), (whole_a, to_a)):
+            move((source,), (bounce,))
+            move((bounce,), (target,))
+
+    @pl.when(jnp.logical_not(over[0] > 0.0))
+    def _():
+        reads, writes = [], []
+        for part in range(4):
+            at = pl.ds(part * quarter, quarter)
+            reads.append(pltpu.make_async_copy(from_r.at[at], bounce.at[at], sem.at[2, part]))
+            reads[-1].start()
+        for part in range(4):
+            at = pl.ds(part * quarter, quarter)
+            writes.append(pltpu.make_async_copy(from_a.at[at], to_a.at[at], sem.at[1, part]))
+            writes[-1].start()
+        for part in range(4):
+            at = pl.ds(part * quarter, quarter)
+            reads[part].wait()
+            writes.append(pltpu.make_async_copy(bounce.at[at], to_r.at[at], sem.at[0, part]))
+            writes[-1].start()
+        for copy in writes:
+            copy.wait()
+
+
+def write(over, packed_way, whole_way):
+    vmem = pl.BlockSpec(memory_space=pltpu.VMEM)
+    far = pl.BlockSpec(memory_space=pltpu.HBM)
+    shape = packed_way[0].shape
+    return tuple(
+        pl.pallas_call(
+            write_kernel,
+            out_shape=[jax.ShapeDtypeStruct(x.shape, x.dtype) for x in packed_way],
+            in_specs=[pl.BlockSpec(memory_space=pltpu.SMEM), far, vmem, far, far],
+            out_specs=[far, far],
+            scratch_shapes=[pltpu.VMEM(shape, BF16), pltpu.SemaphoreType.DMA((3, 4))],
+            compiler_params=pltpu.CompilerParams(vmem_limit_bytes=4_000_000),
+        )(over, *packed_way, *whole_way)
     )
 
 
@@ -911,13 +974,14 @@
     whole = functools.partial(exchange, n_dp, n_group)
     if n_dp % 2 or blocks != 2 or n_dp // 2 * piece != LANES:
         return whole(*args)
-    white_rewards, white_advantage, over = ragged(n_dp, n_group, *args)
-    return lax.cond(
+    white_rewards, white_advantage, over, *unused = ragged(n_dp, n_group, *args)
+    whole_way = lax.cond(
         over[0] > 0.0,
-        lambda kept, args: whole(*args),
-        lambda kept, args: kept,
-        (white_rewards, white_advantage), args,
-    )
+        lambda unused, args: tuple(whole(*args)),
+        lambda unused, args: tuple(unused),
+        unused, args,
+    )
+    return write(over, (white_rewards, white_advantage), whole_way)
 
 
 def solution(mesh):

time: 92 us -> 87.8 us (0.954)
  Pallas kernels: 85.6 us -> 82.9 us
  local copies, waits for them, and re-layouts: 4.63 us -> 2.92 us
    pallas_call x1, Pallas kernels: 85.6 us -> 79.9 us  [ragged(): pl.pallas_call(functools.partial(ragged_kernel, n_dp, n_group, cap), out_...]
    pallas_call x0 -> x1, Pallas kernels: none -> 2.95 us  [write(): pl.pallas_call(write_kernel, out_shape=[jax.ShapeDtypeStruct(x.shape, x.d...]
    unnamed x16 -> x14, local copies, waits for them, and re-layouts: 4.63 us -> 2.92 us
where the time goes in v2:
time: 87.8 us; the launch traced here: 87.6 us
  Pallas kernels  82.9 us (94%)
  local copies, waits for them, and re-layouts  2.92 us (3%)
  between operations  1.58 us (2%)
    pallas_call x1, Pallas kernels, ragged(): pl.pallas_call(functools.partial(ragged_kernel, n_dp, n_group, cap), out_...  79.9 us
    pallas_call x1, Pallas kernels, write(): pl.pallas_call(write_kernel, out_shape=[jax.ShapeDtypeStruct(x.shape, x.d...  2.95 us
    unnamed x14, local copies, waits for them, and re-layouts  2.92 us

profile of v2, /device:TPU:0, one launch (start us, length us, event | category | flops | bytes accessed | tf_op | source)
XLA Modules:
  0.0 87.6 jit_solution(17094957636487165120)
XLA Ops:
  0.6 0.0 copy-start.2
  0.6 0.0 copy-start.3
  0.7 0.0 copy-start.4
  0.7 0.0 copy-start.5
  0.7 0.0 copy-start.6
  0.7 79.9 %shard_map.86 = (bf16[256,4096]{1,0:T(8,128)(2,1)S(1)}, bf16[256,4096]{1,0:T(8,128)(2,1)S(1)}, f32[1]{0:T(128)}, bf16[256,4096]{1,0:T(8,128)(2,1)}, bf16[256,4096]{1,0:T(8,128)(2,1)}) custom-call(bf16[256,4096]{1,0:T(8,128)(2,1)} %rew_hbm.1, bf16[256,4096]{1,0:T(8,128)(2,1)} %val_hbm.1, s32[2,128]{1,0:T(2,128)} %bitcast.7, f32[2,128]{1,0:T(2,128)} %bitcast.11, ...), custom_call_target="tpu_custom_call" | custom-call | tf_op jit(solution)/shard_map/pallas_call | solution.py:879
  80.6 0.0 copy-start
  80.6 1.3 %copy-done = bf16[256,4096]{1,0:T(8,128)(2,1)} copy-done((bf16[256,4096]{1,0:T(8,128)(2,1)}, bf16[256,4096]{1,0:T(8,128)(2,1)S(1)}, u32[]{:S(2)}) %copy-start) | copy-done | bytes 2097176
  82.6 0.0 copy-done.2
  82.6 0.0 copy-done.3
  82.6 0.0 copy-done.4
  82.6 0.0 copy-done.5
  82.7 0.0 copy-done.6
  82.7 0.2 conditional.1
  82.9 0.0 copy-start.1
  82.9 1.6 %copy-done.1 = bf16[256,4096]{1,0:T(8,128)(2,1)S(1)} copy-done((bf16[256,4096]{1,0:T(8,128)(2,1)S(1)}, bf16[256,4096]{1,0:T(8,128)(2,1)}, u32[]{:S(2)}) %copy-start.1) | copy-done | bytes 2097176
  84.5 3.0 %shard_map.87 = (bf16[256,4096]{1,0:T(8,128)(2,1)}, bf16[256,4096]{1,0:T(8,128)(2,1)}) custom-call(f32[1]{0:T(128)} %get-tuple-element.34.over, bf16[256,4096]{1,0:T(8,128)(2,1)S(1)} %get-tuple-element.35.from_r, bf16[256,4096]{1,0:T(8,128)(2,1)S(1)} %copy-done.1, bf16[256,4096]{1,0:T(8,128)(2,1)} %get-tuple-element.39.whole_r, ...), custom_call_target="tpu_custom_call" | custom-call | tf_op jit(solution)/shard_map/pallas_call | solution.py:956
Async XLA Ops:
  0.6 82.0 %copy-start.2 = (s32[256]{0:T(256)S(1)}, s32[256]{0:T(256)}, u32[]{:S(2)}) copy-start(s32[256]{0:T(256)} %param.11) | copy-start | bytes 3076
  0.6 82.0 %copy-start.3 = (s32[2,128]{1,0:T(2,128)S(1)}, s32[2,128]{1,0:T(2,128)}, u32[]{:S(2)}) copy-start(s32[2,128]{1,0:T(2,128)} %perm_hbm.1) | copy-start | bytes 3076
  0.7 82.0 %copy-start.4 = (s32[256]{0:T(256)S(1)}, s32[256]{0:T(256)}, u32[]{:S(2)}) copy-start(s32[256]{0:T(256)} %param.15) | copy-start | bytes 3076
  0.7 82.0 %copy-start.5 = (f32[256]{0:T(256)S(1)}, f32[256]{0:T(256)}, u32[]{:S(2)}) copy-start(f32[256]{0:T(256)} %param.12) | copy-start | bytes 3076
  0.7 82.0 %copy-start.6 = (s32[1,8]{1,0:T(1,128)S(1)}, s32[1,8]{1,0:T(1,128)}, u32[]{:S(2)}) copy-start(s32[1,8]{1,0:T(1,128)} %dest_hbm.1) | copy-start | bytes 100
  80.6 1.3 %copy-start = (bf16[256,4096]{1,0:T(8,128)(2,1)}, bf16[256,4096]{1,0:T(8,128)(2,1)S(1)}, u32[]{:S(2)}) copy-start(bf16[256,4096]{1,0:T(8,128)(2,1)S(1)} %get-tuple-element.36.from_a) | copy-start | bytes 6291460
  82.9 1.6 %copy-start.1 = (bf16[256,4096]{1,0:T(8,128)(2,1)S(1)}, bf16[256,4096]{1,0:T(8,128)(2,1)}, u32[]{:S(2)}) copy-start(bf16[256,4096]{1,0:T(8,128)(2,1)} %copy-done) | copy-start | bytes 6291460

commit v3 on v0

--- a/solution.py
+++ b/solution.py
@@ -138,23 +138,33 @@
 NT = (((1,), (1,)), ((), ()))
 
 
-def exchange_kernel(
-    n_dp, n_group,
-    rbuf, val_hbm, rate_ref, packed,
-    white_r, white_a,
-    out_r, out_a, out_st, out_ch,
-    vbuf, abuf, rsend, asend, tri, lower, upper, lenb, bstep, carry,
-    acc, tbuf, tstage, tsend, trecv, psend, precv, qsend, qrecv, tot,
-    load_sem, own_sem, rs_sem, rr_sem, as_sem, ar_sem, ts_sem, tr_sem, ps_sem, pr_sem, qs_sem, qr_sem,
+def ragged_kernel(
+    n_dp, n_group, own_part, shared,
+    rew_hbm, val_hbm, len_hbm, rate_hbm, dest_hbm, perm_hbm, mini_hbm,
+    white_far, white_a, over_out, unused_r, unused_a,
+    rbuf, vbuf, abuf, white_r, len_v, rate_v, perm_v, mini_v, dest_v,
+    dsend, psend, hsend, hrecv, merged, esend, erecv, dense, packed, chooser, placer, spread,
+    out_st, out_ch, tri, lower, upper, lenb, bstep, carry,
+    acc, tbuf, tstage, tsend, trecv, psum, precv, qsum, qrecv, tot,
+    load_sem, meta_sem, own_sem, ds_sem, dr_sem, ks_sem, kr_sem, hs_sem, hr_sem, fs_sem, xs_sem, xr_sem, es_sem,
+    ts_sem, tr_sem, ps_sem, pr_sem, qs_sem, qr_sem,
 ):
     rows, span = rbuf.shape
     blocks = out_ch.shape[0]
     piece = rows // n_dp
+    half = n_dp // 2
+    chunks = span // LANES
+    quarter = half // 2
+    depth = own_part + shared
     wide = tri.shape[0]
-    cuts = ((0, span // 2), (span // 2, 3 * span // 8), (7 * span // 8, span // 8))
+    cuts = part_cuts(own_part)
     me = lax.axis_index("dp")
     mine = lax.axis_index("group")
-    order = sorted(range(1, n_dp), key=lambda d: (abs(2 * d - n_dp), d))
+    side = me // half
+    spot = lax.rem(me, half)
+    column = lax.rem(spot, quarter)
+    core = lax.rem(mine, 2)
+    partner = mine + 1 - 2 * core
 
     def dp_peer(d):
         return lax.rem(me + d, n_dp)
@@ -162,15 +172,26 @@
     def group_peer(d):
         return lax.rem(mine + d, n_group)
 
-    quarter = rows // 4
+    def near(j):
+        return side * half + lax.rem(me + j, half)
+
+    def across(i, f):
+        level = side if f == 0 else 1 - side
+        return (1 - side) * half + level * quarter + lax.rem(column + i, quarter)
+
+    small = []
+    for i, (src, dst) in enumerate(
+        ((len_hbm, len_v), (dest_hbm, dest_v), (rate_hbm, rate_v), (perm_hbm, perm_v), (mini_hbm, mini_v))
+    ):
+        small.append(pltpu.make_async_copy(src, dst, meta_sem.at[i]))
+        small[-1].start()
+    step = rows // 4
     loads = []
-    for part in range(4):
-        at = pl.ds(part * quarter, quarter)
-        loads.append(pltpu.make_async_copy(val_hbm.at[at], vbuf.at[at], load_sem.at[part]))
-        loads[-1].start()
-
-    def row_of(kind, b):
-        return packed[kind * blocks + b : kind * blocks + b + 1, :].astype(F32)
+    for x, (src, dst) in enumerate(((rew_hbm, rbuf), (val_hbm, vbuf))):
+        for part in range(4):
+            at = pl.ds(part * step, step)
+            loads.append(pltpu.make_async_copy(src.at[at], dst.at[at], load_sem.at[x, part]))
+            loads[-1].start()
 
     barrier = pltpu.get_barrier_semaphore()
     for d in range(1, n_dp):
@@ -178,23 +199,72 @@
     for d in range(1, n_group):
         pl.semaphore_signal(barrier, inc=1, device_id=(me, group_peer(d)), device_id_type=MESH)
 
-    targets = [
-        jnp.broadcast_to(row_of(3, 0)[:, p : p + 1], (piece, LANES)) for p in range(n_dp)
-    ]
-
-    def pick(d, source):
-        k = jnp.full((piece, LANES), dp_peer(d), jnp.int32).astype(F32)
+    lane = lax.broadcasted_iota(jnp.int32, (LANES, LANES), 1)
+    sub = lax.broadcasted_iota(jnp.int32, (LANES, LANES), 0)
+    before = jnp.logical_and(sub // piece == lane // piece, sub < lane).astype(F32).astype(BF16)
+    per_vreg = LANES // piece
+
+    def used(length):
+        return ((length + (LANES - 1)) // LANES).astype(F32).astype(BF16)
+
+    for copy in small:
+        copy.wait()
+
+    dests = [dest_v[0:1, p : p + 1] for p in range(n_dp)]
+    targets = [jnp.broadcast_to(dest.astype(F32), (piece, LANES)) for dest in dests]
+    row_dest = []
+    for b in range(blocks):
+        here = jnp.zeros((16, LANES), jnp.int32)
+        for q in range(per_vreg):
+            here = jnp.where(lane[0:16] // piece == q, dests[b * per_vreg + q], here)
+        row_dest.append(here)
+    fold = (sub % piece == lane % piece).astype(F32).astype(BF16)
+
+    def pick(k, source):
+        k = jnp.full((piece, LANES), k, jnp.int32).astype(F32)
         weights = [(target == k).astype(F32).astype(source.dtype) for target in targets]
         for c in range(0, source.shape[1], LANES):
             at = slice(c, c + LANES)
             yield at, sum(source[p * piece : (p + 1) * piece, at] * weights[p] for p in range(n_dp))
 
-    def stage(d, source, target):
-        for at, part in pick(d, source):
-            target[d, :, at] = part
-
-    stage(order[0], rbuf, rsend)
-    pl.semaphore_wait(barrier, n_dp + n_group - 2)
+    def mirrored(key):
+        return jnp.where(key >= own_part, own_part + depth - 1 - key, key)
+
+    core_row = jnp.full((1, LANES), core, jnp.int32)
+
+    def choose(i, f):
+        wanted = jnp.zeros((16, LANES), F32)
+        for b in range(blocks):
+            here = jnp.broadcast_to(len_v[b : b + 1, :], (16, LANES))
+            here = jnp.where(row_dest[b] == across(i, f), here, 0)
+            wanted = wanted + jnp.dot(used(here), fold, preferred_element_type=F32)
+        base = jnp.dot(wanted.astype(BF16), before, preferred_element_type=F32)
+        taken = jnp.max((base + wanted)[0:8], axis=1, keepdims=True)
+        base = base.astype(jnp.int32)[0:1]
+        wanted = wanted.astype(jnp.int32)[0:1]
+        place = lax.broadcasted_iota(jnp.int32, (depth, LANES), 0)
+        for v in range(chunks // per_vreg):
+            c = lane[0:1] // piece + v * per_vreg
+            key = base + c
+            key = jnp.where(core_row == i, key, mirrored(key))
+            key = jnp.where(c < wanted, key, -1)
+            at = slice(v * LANES, (v + 1) * LANES)
+            chooser[i, f, :, at] = (place == key).astype(F32).astype(BF16)
+        return jnp.maximum(jnp.broadcast_to(taken, (8, LANES)) - own_part, 0.0)
+
+    def pack(x, i, f, source):
+        arranged = jnp.concatenate([part for _, part in pick(across(i, f), source)], axis=0)
+        got = jnp.dot(chooser[i, f], arranged, preferred_element_type=F32).astype(BF16)
+        psend[x, i, f] = got[:own_part]
+        if shared:
+            hsend[x, i, f] = got[own_part:]
+
+    def copy_dense(x, j, source):
+        for at, part in pick(near(j), source):
+            dsend[x, j, :, at] = part
+
+    for load in loads[:4]:
+        load.wait()
 
     def remote(src, dst, send, recv, who):
         return pltpu.make_async_remote_copy(
@@ -202,34 +272,119 @@
             device_id=who, device_id_type=MESH,
         )
 
+    def dense_copy(x, j):
+        return remote(
+            dsend.at[x, j], dense.at[x, spot], ds_sem.at[x, j], dr_sem.at[x, j], (near(j), mine)
+        )
+
+    def packed_copy(x, i, f, part):
+        at = pl.ds(*cuts[x][part])
+        return remote(
+            psend.at[x, i, f, at], packed.at[x, spot, at],
+            ks_sem.at[x, part, i, f], kr_sem.at[x, part, spot], (across(i, f), mine),
+        )
+
+    last = pl.ds(own_part, shared)
+
+    def swap_copy(x, f):
+        return remote(
+            hsend.at[x, 1 - core, f], hrecv.at[x, f], xs_sem.at[x, f], xr_sem.at[x, f], (me, partner)
+        )
+
+    def shared_copy(x, f):
+        return remote(
+            merged.at[x, f], packed.at[x, spot, last],
+            hs_sem.at[x, f], hr_sem.at[x, spot], (across(core, f), mine),
+        )
+
+    def relay_copy(x, f, own):
+        q = f * quarter + lax.rem(column + core + (0 if own else 1), 2)
+        return remote(
+            packed.at[x, q, last], packed.at[x, q, last],
+            fs_sem.at[x, f], hr_sem.at[x, q], (me, partner),
+        )
+
+    def swap(x):
+        for f in range(2 if shared else 0):
+            swap_copy(x, f).start()
+
+    def merge(x):
+        for f in range(2 if shared else 0):
+            swap_copy(x, f).wait_recv()
+            merged[x, f] = hsend[x, core, f] + hrecv[x, f]
+        for f in range(2 if shared else 0):
+            shared_copy(x, f).start()
+
+    def receive_packed(x, part):
+        at = pl.ds(*cuts[x][part])
+        for q in range(half):
+            remote(
+                psend.at[x, 0, 0, at], packed.at[x, q, at],
+                ks_sem.at[x, part, 0, 0], kr_sem.at[x, part, q], (across(0, 0), mine),
+            ).wait_recv()
+
+    def relay(x):
+        for f in range(2 if shared else 0):
+            relay_copy(x, f, True).wait_recv()
+            relay_copy(x, f, True).start()
+
+    def relayed(x):
+        for f in range(2 if shared else 0):
+            relay_copy(x, f, False).wait_recv()
+
+    order = []
+    for i in range(quarter):
+        for f in range(2):
+            order.append(("own", i, f))
+            if len(order) < n_dp - 1:
+                order.append(("near", i * 2 + f + 1, 0))
+    beyond_own = {}
+
+    def stage(item):
+        kind, i, f = item
+        if kind == "near":
+            copy_dense(0, i, rbuf)
+        else:
+            beyond_own[i, f] = choose(i, f)
+            pack(0, i, f, rbuf)
+
     sent = []
-    second = []
-    for d, later in zip(order, order[1:] + [0]):
-        stage(later, rbuf, rsend)
-        k = dp_peer(d)
-        sent.append(remote(rsend.at[d], out_r.at[me], rs_sem.at[d], rr_sem.at[d], (k, mine)))
-        sent[-1].start()
-    own = [pltpu.make_async_copy(rsend.at[0], out_r.at[me], own_sem.at[0])]
-    own[0].start()
+
+    def issue(x, item):
+        kind, i, f = item
+        if kind == "near":
+            dense_sent[x].append(dense_copy(x, i))
+            dense_sent[x][-1].start()
+        else:
+            sent.append(packed_copy(x, i, f, 0))
+            sent[-1].start()
+
+    dense_sent = [[], []]
+    stage(order[0])
+    pl.semaphore_wait(barrier, n_dp + n_group - 2)
+    held = len(order) - 2
+    for item, later in zip(order[:held], order[1:]):
+        stage(later)
+        issue(0, item)
 
     for b in range(blocks):
         at = pl.ds(b * LANES, LANES)
-        rate = jnp.transpose(jnp.broadcast_to(rate_ref[b : b + 1, :], (LANES, LANES)))
-        length = jnp.transpose(jnp.broadcast_to(row_of(0, b), (LANES, LANES)))
+        rate = jnp.transpose(jnp.broadcast_to(rate_v[b : b + 1, :], (LANES, LANES)))
+        length = jnp.transpose(jnp.broadcast_to(len_v[b : b + 1, :].astype(F32), (LANES, LANES)))
         lenb[at, :] = length.astype(jnp.int32)
         bstep[at, :] = jnp.exp(-rate * wide)
         carry[at, :] = jnp.zeros((LANES, LANES), F32)
         for x in range(4):
             acc[x, at, :] = jnp.zeros((LANES, LANES), F32)
-        for h in range(wide // LANES):
-            offset = (lax.broadcasted_iota(jnp.int32, (LANES, LANES), 1) + h * LANES).astype(F32)
-            lower[at, h * LANES : (h + 1) * LANES] = jnp.exp(-rate * offset)
-            upper[at, h * LANES : (h + 1) * LANES] = jnp.exp(rate * offset)
+        for i in range(wide // LANES):
+            offset = (lane + i * LANES).astype(F32)
+            lower[at, i * LANES : (i + 1) * LANES] = jnp.exp(-rate * offset)
+            upper[at, i * LANES : (i + 1) * LANES] = jnp.exp(rate * offset)
     tri[...] = (
         lax.broadcasted_iota(jnp.int32, (wide, wide), 0)
         >= lax.broadcasted_iota(jnp.int32, (wide, wide), 1)
     ).astype(F32).astype(BF16)
-    for load in loads:
+    for load in loads[4:]:
         load.wait()
 
     reps = wide // LANES
@@ -256,12 +411,11 @@
             abuf[at, pl.ds(col, wide)] = a
             a = a.astype(F32)
             for x, term in enumerate((r, a, r * r, a * a)):
-                acc[x, at, :] += sum(term[:, h * LANES : (h + 1) * LANES] for h in range(reps))
+                acc[x, at, :] += sum(term[:, i * LANES : (i + 1) * LANES] for i in range(reps))
         return 0
 
     lax.fori_loop(0, span // wide, column_step, 0)
 
-    lane = lax.broadcasted_iota(jnp.int32, (LANES, LANES), 1)
     for b in range(blocks):
         at = pl.ds(b * LANES, LANES)
         terms = jnp.where(lane == 0, lenb[at, :].astype(F32), 0.0)
@@ -271,48 +425,52 @@
         tbuf[at, :] = terms
     tstage[...] = jnp.zeros_like(tstage)
 
-    def stage_second(d, _):
-        stage(d, abuf, asend)
-        for at, part in pick(d, tbuf):
+    def stage_terms(d, _):
+        for at, part in pick(dp_peer(d), tbuf):
             tstage[0:piece, :] = part
         tsend[d] = jnp.transpose(tstage[...])[0:8, :]
         return 0
 
-    lax.fori_loop(0, n_dp, stage_second, 0)
+    lax.fori_loop(0, n_dp, stage_terms, 0)
 
     terms_sent = []
-    for d in order:
+    for d in range(1, n_dp):
         k = dp_peer(d)
         terms_sent.append(remote(tsend.at[d], trecv.at[me], ts_sem.at[d], tr_sem.at[d], (k, mine)))
         terms_sent[-1].start()
     trecv[me] = tsend[0]
-
-    def send_second(part):
-        at = pl.ds(*cuts[part])
-        second.append([])
-        for d in order:
-            k = dp_peer(d)
-            second[part].append(
-                remote(
-                    asend.at[d, :, at], out_a.at[me, :, at],
-                    as_sem.at[part, d], ar_sem.at[part, d], (k, mine),
-                )
-            )
-            second[part][-1].start()
-
-    send_second(0)
-    own.append(pltpu.make_async_copy(asend.at[0], out_a.at[me], own_sem.at[1]))
-    own[1].start()
+    for item, later in zip(order[held:], order[held + 1 :] + [("near", 0, 0)]):
+        stage(later)
+        issue(0, item)
+    own = [pltpu.make_async_copy(dsend.at[0, 0], dense.at[0, spot], own_sem.at[0])]
+    own[0].start()
+    swap(0)
+    for i in range(quarter):
+        for f in range(2):
+            esend[2 * i + f] = beyond_own[i, f]
+    for i in range(quarter):
+        for f in range(2):
+            pack(1, i, f, abuf)
+    for j in range(half):
+        copy_dense(1, j, abuf)
+    swap(1)
+    merge(0)
+    tell = remote(esend, erecv, es_sem.at[0], es_sem.at[1], (me, partner))
+    tell.start()
 
     for copy in terms_sent:
         copy.wait()
 
-    row = lax.broadcasted_iota(jnp.int32, (LANES, LANES), 0).astype(F32)
-    partial = jnp.zeros((8, LANES), F32)
+    row = sub.astype(F32)
+    over = jnp.zeros((8, LANES), F32)
+    tell.wait()
+    for slot in range(half):
+        over = jnp.where(esend[slot] + erecv[slot] > shared, 1.0, over)
+    partial = jnp.where(lax.broadcasted_iota(jnp.int32, (8, LANES), 0) == 5, over, 0.0)
     per_block = LANES // piece
     for b in range(blocks):
-        picked = (row == row_of(1, b)).astype(F32)
-        member = (row == row_of(2, b)).astype(F32)
+        picked = (row == perm_v[b : b + 1, :].astype(F32)).astype(F32)
+        member = (row == mini_v[b : b + 1, :].astype(F32)).astype(F32)
         arrived_member = lax.dot_general(
             member.astype(BF16), picked.astype(BF16), NT, preferred_element_type=F32
         )
@@ -324,34 +482,92 @@
         )
         out_ch[b] = jnp.transpose(picked).astype(BF16)
         tot[b] = jnp.dot(terms, picked, precision=HIGHEST, preferred_element_type=F32)
-    psend[...] = partial
+    psum[...] = partial
     precv[me] = partial
     sums_sent = []
-    for d in order:
+    for d in range(1, n_dp):
         k = dp_peer(d)
-        sums_sent.append(remote(psend, precv.at[me], ps_sem.at[d], pr_sem.at[d], (k, mine)))
+        sums_sent.append(remote(psum, precv.at[me], ps_sem.at[d], pr_sem.at[d], (k, mine)))
         sums_sent[-1].start()
 
-    for part in range(1, len(cuts)):
-        send_second(part)
+    merge(1)
+    for item in order:
+        issue(1, item)
+    own.append(pltpu.make_async_copy(dsend.at[1, 0], dense.at[1, spot], own_sem.at[1]))
+    own[1].start()
+    for part in range(1, len(cuts[1])):
+        for i in range(quarter):
+            for f in range(2):
+                sent.append(packed_copy(1, i, f, part))
+                sent[-1].start()
+
+    relay(0)
+    other = 1 - side
+    length = trecv[other * per_block]
+    for s in range(1, per_block):
+        length = length + pltpu.roll(trecv[other * per_block + s], s * piece, 1)
+    length = jnp.broadcast_to(length[0:1], (16, LANES)).astype(jnp.int32)
+    wanted = used(length)
+    base = jnp.dot(wanted, before, preferred_element_type=F32)
+    base = jnp.transpose(jnp.broadcast_to(base[0:1], (LANES, LANES))).astype(jnp.int32)
+    wanted = jnp.transpose(jnp.broadcast_to(wanted.astype(F32)[0:1], (LANES, LANES))).astype(jnp.int32)
+
+    flips = lax.rem(sub // piece + column, 2) != core
+
+    def place_chunk(c, _):
+        key = base + c
+        key = jnp.where(flips, mirrored(key), key)
+        key = jnp.where(c < wanted, key, -1)
+        at = pl.ds(pl.multiple_of(c * piece, piece), piece)
+        for n in range(depth // LANES):
+            match = (lane + n * LANES == key).astype(F32).astype(BF16)
+            for q in range(half):
+                placer[q, at, n * LANES : (n + 1) * LANES] = match[q * piece : (q + 1) * piece]
+        return 0
+
+    lax.fori_loop(0, chunks, place_chunk, 0)
+
+    def unpack(x, start, stop, first):
+        stop = depth if stop == own_part else stop
+
+        def one(q, _):
+            got = jnp.dot(
+                placer[q, :, start:stop], packed[x, q, start:stop, :], preferred_element_type=F32
+            ).astype(BF16)
+            at = pl.ds(pl.multiple_of(q * piece, piece), piece)
+            for c in range(chunks):
+                cols = slice(c * LANES, (c + 1) * LANES)
+                part = got[c * piece : (c + 1) * piece]
+                spread[x, at, cols] = part if first else spread[x, at, cols] + part
+            return 0
+
+        lax.fori_loop(0, half, one, 0)
+
+    for copy in own[:1] + dense_sent[0]:
+        copy.wait()
+    receive_packed(0, 0)
+    relayed(0)
+    unpack(0, 0, own_part, True)
+    relay(1)
 
     for copy in sums_sent:
         copy.wait()
     partial = precv[0]
     for k in range(1, n_dp):
         partial = partial + precv[k]
-    qsend[...] = partial
+    qsum[...] = partial
     qrecv[mine] = partial
     group_sent = []
     for d in range(1, n_group):
         k = group_peer(d)
-        group_sent.append(remote(qsend, qrecv.at[mine], qs_sem.at[d], qr_sem.at[d], (me, k)))
+        group_sent.append(remote(qsum, qrecv.at[mine], qs_sem.at[d], qr_sem.at[d], (me, k)))
         group_sent[-1].start()
     for copy in group_sent:
         copy.wait()
     total = qrecv[0]
     for k in range(1, n_group):
         total = total + qrecv[k]
+    over_out[0] = jnp.max(total[5:6, :])
 
     count = jnp.maximum(total[0:1, :], 1.0)
     means = total[1:3, :] / count
@@ -360,99 +576,200 @@
     table = jnp.concatenate([means, scales, jnp.zeros((4, LANES), F32)], axis=0)
     for b in range(blocks):
         at = pl.ds(b * LANES, LANES)
-        member = (row == row_of(2, b)).astype(F32)
+        member = (row == mini_v[b : b + 1, :].astype(F32)).astype(F32)
         here = jnp.dot(table, member, precision=HIGHEST, preferred_element_type=F32)
         here = jnp.concatenate(
             [here[0:4, :], tot[b, 0:1, :], jnp.zeros((LANES - 5, LANES), F32)], axis=0
         )
         out_st[at, :] = jnp.transpose(here)
 
-    def whiten_part(x, source, target, start, width):
-        tile = min(512, width)
+    def whiten_block(x, arrived_at, b, target):
+        tile = 512
 
         def tile_step(i, _):
-            col = pl.multiple_of(start + i * tile, tile)
-            for b in range(blocks):
-                at = pl.ds(b * LANES, LANES)
-                stats = out_st[at, :]
-                position = (col + lax.broadcasted_iota(jnp.int32, (LANES, tile), 1)).astype(F32)
-                arrived = source[b * per_block : (b + 1) * per_block, :, pl.ds(col, tile)]
-                moved = jnp.dot(
-                    out_ch[b], arrived.reshape(LANES, tile), preferred_element_type=F32
-                )
-                white = (moved - stats[:, x : x + 1]) * stats[:, x + 2 : x + 3]
-                white = jnp.where(position < stats[:, 4:5], white, 0.0)
-                target[at, pl.ds(col, tile)] = white.astype(BF16)
+            col = pl.multiple_of(i * tile, tile)
+            at = pl.ds(pl.multiple_of(b * LANES, LANES), LANES)
+            stats = out_st[at, :]
+            position = (col + lax.broadcasted_iota(jnp.int32, (LANES, tile), 1)).astype(F32)
+            moved = jnp.dot(out_ch[b], arrived_at(pl.ds(col, tile)), preferred_element_type=F32)
+            white = (moved - stats[:, x : x + 1]) * stats[:, x + 2 : x + 3]
+            white = jnp.where(position < stats[:, 4:5], white, 0.0)
+            target[at, pl.ds(col, tile)] = white.astype(BF16)
             return 0
 
-        lax.fori_loop(0, width // tile, tile_step, 0)
-
-    for copy in own + sent:
+        lax.fori_loop(0, span // tile, tile_step, 0)
+
+    def whiten_dense(x, target):
+        whiten_block(x, lambda at: dense[x, :, :, at].reshape(LANES, at.size), side, target)
+
+    def whiten_packed(x, target):
+        whiten_block(x, lambda at: spread[x, :, at], other, target)
+
+    whiten_dense(0, white_r)
+    whiten_packed(0, white_r)
+    kept = pltpu.make_async_copy(white_r, white_far.at[pl.ds(0, rows)], own_sem.at[2])
+    kept.start()
+    for copy in own[1:] + dense_sent[1]:
         copy.wait()
-    whiten_part(0, out_r, white_r, 0, span)
-    for part, copies in enumerate(second):
-        for copy in copies:
-            copy.wait_recv()
-        whiten_part(1, out_a, white_a, *cuts[part])
-    for copies in second:
-        for copy in copies:
-            copy.wait_send()
-
-
-def exchange(n_dp, n_group, rewards, values, lengths, decay_rate, piece_dest, row_perm, minibatch):
+    whiten_dense(1, white_a)
+    for part, (start, size) in enumerate(cuts[1]):
+        receive_packed(1, part)
+        if part == len(cuts[1]) - 1:
+            relayed(1)
+        unpack(1, start, start + size, part == 0)
+    whiten_packed(1, white_a)
+    for copy in sent:
+        copy.wait_send()
+    for x in range(2):
+        for f in range(2 if shared else 0):
+            swap_copy(x, f).wait_send()
+            shared_copy(x, f).wait_send()
+            relay_copy(x, f, True).wait_send()
+    kept.wait()
+
+
+def part_cuts(size):
+    a, b = size // 256 * 128, (size - 1) // 128 * 128
+    return (((0, size),), ((0, a), (a, b - a), (b, size - b)))
+
+
+def ragged(n_dp, n_group, own_part, shared, collective_id, spare, rewards, values, lengths, decay_rate, piece_dest, row_perm, minibatch):
     rows, span = rewards.shape
     blocks, block = row_perm.shape
     piece = rows // n_dp
+    half = n_dp // 2
     wide = 256
+    depth = own_part + shared
+    extra = max(shared, 16)
+    chunks = piece * (span // LANES)
     vmem = pl.BlockSpec(memory_space=pltpu.VMEM)
     far = pl.BlockSpec(memory_space=pltpu.HBM)
     dma = pltpu.SemaphoreType.DMA
     whole = pltpu.VMEM((rows, span), BF16)
-    staged = pltpu.VMEM((n_dp, piece, span), BF16)
     factor = pltpu.VMEM((rows, wide), F32)
     column = pltpu.VMEM((rows, LANES), F32)
     small = pltpu.VMEM((n_dp, 8, LANES), F32)
     one = pltpu.VMEM((8, LANES), F32)
+    meta = pltpu.VMEM((blocks, LANES), jnp.int32)
+    dense = pltpu.VMEM((2, half, piece, span), BF16)
+    parts = len(part_cuts(own_part)[1])
     return pl.pallas_call(
-        functools.partial(exchange_kernel, n_dp, n_group),
-        out_shape=(jax.ShapeDtypeStruct((rows, span), BF16),) * 2,
-        in_specs=[vmem, far, vmem, vmem],
-        out_specs=(vmem, vmem),
+        functools.partial(ragged_kernel, n_dp, n_group, own_part, shared),
+        out_shape=tuple(jax.ShapeDtypeStruct((k * rows, span), BF16) for k in (spare, 1))
+        + (jax.ShapeDtypeStruct((1,), F32),)
+        + (jax.ShapeDtypeStruct((rows, span), BF16),) * 2,
+        in_specs=[far] * 7,
+        out_specs=(far, vmem, pl.BlockSpec(memory_space=pltpu.SMEM), far, far),
         scratch_shapes=[
-            staged, staged, column, pltpu.VMEM((blocks, LANES, LANES), BF16),
-            whole, whole, staged, staged,
+            whole, whole, whole, whole, meta, pltpu.VMEM((blocks, LANES), F32), meta, meta,
+            pltpu.VMEM((1, n_dp), jnp.int32),
+            dense, pltpu.VMEM((2, half // 2, 2, own_part, LANES), BF16),
+            pltpu.VMEM((2, 2, 2, extra, LANES), BF16),
+            pltpu.VMEM((2, 2, extra, LANES), BF16), pltpu.VMEM((2, 2, extra, LANES), BF16),
+            pltpu.VMEM((half, 8, LANES), F32), pltpu.VMEM((half, 8, LANES), F32),
+            dense, pltpu.VMEM((2, half, depth, LANES), BF16),
+            pltpu.VMEM((half // 2, 2, depth, chunks), BF16), pltpu.VMEM((half, chunks, depth), BF16),
+            pltpu.VMEM((2, LANES, span), BF16),
+            column, pltpu.VMEM((blocks, LANES, LANES), BF16),
             pltpu.VMEM((wide, wide), BF16), factor, factor,
             pltpu.VMEM((rows, LANES), jnp.int32), column, column,
             pltpu.VMEM((4, rows, LANES), F32), column, pltpu.VMEM((LANES, LANES), F32),
             small, small, one, small, one, pltpu.VMEM((n_group, 8, LANES), F32),
             pltpu.VMEM((blocks, 8, LANES), F32),
-            dma((4,)), dma((2,)), dma((n_dp,)), dma((n_dp,)), dma((3, n_dp)), dma((3, n_dp)),
+            dma((2, 4)), dma((5,)), dma((3,)), dma((2, half)), dma((2, half)),
+            dma((2, parts, half // 2, 2)), dma((2, parts, half)),
+            dma((2, 2)), dma((2, half)), dma((2, 2)), dma((2, 2)), dma((2, 2)), dma((2,)),
             dma((n_dp,)), dma((n_dp,)), dma((n_dp,)), dma((n_dp,)), dma((n_group,)), dma((n_group,)),
         ],
         compiler_params=pltpu.CompilerParams(
-            collective_id=0, has_side_effects=True, vmem_limit_bytes=50_000_000
+            collective_id=collective_id, has_side_effects=True, vmem_limit_bytes=52_000_000
         ),
     )(
-        rewards, values, decay_rate.reshape(blocks, block),
-        jnp.concatenate(
-            [
-                lengths.reshape(blocks, block),
-                row_perm,
-                minibatch.reshape(blocks, block),
-                jnp.pad(piece_dest, ((0, 0), (0, block - piece_dest.shape[1]))),
-            ],
-            axis=0,
-        ),
+        rewards, values, lengths.reshape(blocks, block), decay_rate.reshape(blocks, block),
+        piece_dest, row_perm, minibatch.reshape(blocks, block),
+    )
+
+
+def write_kernel(over, from_r, from_a, whole_r, whole_a, to_r, to_a, bounce, sem):
+    quarter = from_a.shape[0] // 4
+
+    def move(sources, targets):
+        copies = []
+        for x, (src, dst) in enumerate(zip(sources, targets)):
+            for part in range(4):
+                at = pl.ds(part * quarter, quarter)
+                copies.append(pltpu.make_async_copy(src.at[at], dst.at[at], sem.at[x, part]))
+                copies[-1].start()
+        for copy in copies:
+            copy.wait()
+
+    @pl.when(over[0] > 0.0)
+    def _():
+        for source, target in ((whole_r, to_r), (whole_a, to_a)):
+            move((source,), (bounce,))
+            move((bounce,), (target,))
+
+    @pl.when(jnp.logical_not(over[0] > 0.0))
+    def _():
+        reads, writes = [], []
+        for part in range(4):
+            at = pl.ds(part * quarter, quarter)
+            reads.append(pltpu.make_async_copy(from_r.at[at], bounce.at[at], sem.at[2, part]))
+            reads[-1].start()
+        for part in range(4):
+            at = pl.ds(part * quarter, quarter)
+            writes.append(pltpu.make_async_copy(from_a.at[at], to_a.at[at], sem.at[1, part]))
+            writes[-1].start()
+        for part in range(4):
+            at = pl.ds(part * quarter, quarter)
+            reads[part].wait()
+            writes.append(pltpu.make_async_copy(bounce.at[at], to_r.at[at], sem.at[0, part]))
+            writes[-1].start()
+        for copy in writes:
+            copy.wait()
+
+
+def write(over, packed_way, whole_way):
+    vmem = pl.BlockSpec(memory_space=pltpu.VMEM)
+    far = pl.BlockSpec(memory_space=pltpu.HBM)
+    shape = packed_way[1].shape
+    return tuple(
+        pl.pallas_call(
+            write_kernel,
+            out_shape=[jax.ShapeDtypeStruct(x.shape, x.dtype) for x in whole_way],
+            in_specs=[pl.BlockSpec(memory_space=pltpu.SMEM), far, vmem, far, far],
+            out_specs=[far, far],
+            scratch_shapes=[pltpu.VMEM(shape, BF16), pltpu.SemaphoreType.DMA((3, 4))],
+            compiler_params=pltpu.CompilerParams(vmem_limit_bytes=52_000_000),
+        )(over, *packed_way, *whole_way)
     )
 
 
 def local(n_dp, n_group, rewards, values, lengths, decay_rate, piece_dest, row_perm, minibatch):
     rows, span = rewards.shape
-    if (rows // n_dp) % 16 or LANES % (rows // n_dp) or row_perm.shape[1] != LANES or span % 4096:
-        return plain_local(rewards, values, lengths, decay_rate, piece_dest, row_perm, minibatch)
-    return exchange(
-        n_dp, n_group, rewards, values, lengths, decay_rate, piece_dest, row_perm, minibatch
-    )
+    blocks, block = row_perm.shape
+    piece = rows // n_dp
+    args = (rewards, values, lengths, decay_rate, piece_dest, row_perm, minibatch)
+    if piece % 16 or LANES % piece or block != LANES or span % 4096:
+        return plain_local(*args)
+    if n_dp // 4 != 2 or n_dp % 4 or n_group % 2 or blocks != 2 or n_dp // 2 * piece != LANES:
+        return plain_local(*args)
+    chunks = piece * (span // LANES)
+    own_part, shared = chunks * 9 // 16, chunks * 3 // 16
+
+    def whole(results):
+        return results[0][:rows], results[1]
+
+    white_rewards, white_advantage, over, *unused = ragged(
+        n_dp, n_group, own_part, shared, 0, 8, *args
+    )
+    whole_way = lax.cond(
+        over[0] > 0.0,
+        lambda unused, args: whole(ragged(n_dp, n_group, chunks, 0, 1, 1, *args)),
+        lambda unused, args: tuple(unused),
+        unused, args,
+    )
+    return write(over, (white_rewards, white_advantage), whole_way)
 
 
 def solution(mesh):

time: 106 us -> 80.7 us (0.76)
  Pallas kernels: 99.6 us -> 78.7 us
  local copies, waits for them, and re-layouts: 4.91 us -> 0.02 us
    pallas_call x1 -> x2, Pallas kernels: 99.6 us -> 78.7 us  [the longest x1 74.8 us: ragged(): pl.pallas_call(functools.partial(ragged_kernel, n_dp, n_group, own_part,...]
    unnamed x6 -> x10, local copies, waits for them, and re-layouts: 4.91 us -> 0.02 us
where the time goes in v3:
time: 80.7 us; the launch traced here: 80.5 us
  Pallas kernels  78.7 us (98%)
  between operations  1.55 us (2%)
    pallas_call x1, Pallas kernels, ragged(): pl.pallas_call(functools.partial(ragged_kernel, n_dp, n_group, own_part,...  74.8 us
    pallas_call x1, Pallas kernels, write(): pl.pallas_call(write_kernel, out_shape=[jax.ShapeDtypeStruct(x.shape, x.d...  3.83 us

profile of v3, /device:TPU:0, one launch (start us, length us, event | category | flops | bytes accessed | tf_op | source)
XLA Modules:
  0.0 80.5 jit_solution(15212329864285657224)
XLA Ops:
  0.6 0.0 copy-start
  0.6 0.0 copy-start.1
  0.7 0.0 copy-start.2
  0.7 0.0 copy-start.3
  0.7 0.0 copy-start.4
  0.7 74.8 %shard_map.86 = (bf16[2048,4096]{1,0:T(8,128)(2,1)}, bf16[256,4096]{1,0:T(8,128)(2,1)S(1)}, f32[1]{0:T(128)}, bf16[256,4096]{1,0:T(8,128)(2,1)}, bf16[256,4096]{1,0:T(8,128)(2,1)}) custom-call(bf16[256,4096]{1,0:T(8,128)(2,1)} %rew_hbm.1, bf16[256,4096]{1,0:T(8,128)(2,1)} %val_hbm.1, s32[2,128]{1,0:T(2,128)} %bitcast.7, f32[2,128]{1,0:T(2,128)} %bitcast.9, ...), custom_call_target="tpu_custom_call" | custom-call | tf_op jit(solution)/shard_map/pallas_call | solution.py:656
  76.2 0.0 copy-done
  76.2 0.0 copy-done.1
  76.2 0.0 copy-done.2
  76.2 0.0 copy-done.3
  76.2 0.0 copy-done.4
  76.2 0.3 conditional.1
  76.5 3.8 %shard_map.87 = (bf16[256,4096]{1,0:T(8,128)(2,1)}, bf16[256,4096]{1,0:T(8,128)(2,1)}) custom-call(f32[1]{0:T(128)} %get-tuple-element.36.over, bf16[2048,4096]{1,0:T(8,128)(2,1)} %get-tuple-element.37.from_r, bf16[256,4096]{1,0:T(8,128)(2,1)S(1)} %get-tuple-element.38.from_a, bf16[256,4096]{1,0:T(8,128)(2,1)} %get-tuple-element.41.whole_r, ...), custom_call_target="tpu_custom_call" | custom-call | tf_op jit(solution)/shard_map/pallas_call | solution.py:737
Async XLA Ops:
  0.6 75.5 %copy-start = (s32[256]{0:T(256)S(1)}, s32[256]{0:T(256)}, u32[]{:S(2)}) copy-start(s32[256]{0:T(256)} %param.11) | copy-start | bytes 3076
  0.6 75.5 %copy-start.1 = (f32[256]{0:T(256)S(1)}, f32[256]{0:T(256)}, u32[]{:S(2)}) copy-start(f32[256]{0:T(256)} %param.12) | copy-start | bytes 3076
  0.7 75.5 %copy-start.2 = (s32[2,128]{1,0:T(2,128)S(1)}, s32[2,128]{1,0:T(2,128)}, u32[]{:S(2)}) copy-start(s32[2,128]{1,0:T(2,128)} %perm_hbm.1) | copy-start | bytes 3076
  0.7 75.5 %copy-start.3 = (s32[256]{0:T(256)S(1)}, s32[256]{0:T(256)}, u32[]{:S(2)}) copy-start(s32[256]{0:T(256)} %param.15) | copy-start | bytes 3076
  0.7 75.5 %copy-start.4 = (s32[1,8]{1,0:T(1,128)S(1)}, s32[1,8]{1,0:T(1,128)}, u32[]{:S(2)}) copy-start(s32[1,8]{1,0:T(1,128)} %dest_hbm.1) | copy-start | bytes 100

commit v4 on v3

--- a/solution.py
+++ b/solution.py
@@ -141,12 +141,12 @@
 def ragged_kernel(
     n_dp, n_group, own_part, shared,
     rew_hbm, val_hbm, len_hbm, rate_hbm, dest_hbm, perm_hbm, mini_hbm,
-    white_far, white_a, over_out, unused_r, unused_a,
+    white_far, white_a, white_k, over_out, unused_r, unused_a,
     rbuf, vbuf, abuf, white_r, len_v, rate_v, perm_v, mini_v, dest_v,
-    dsend, psend, hsend, hrecv, merged, esend, erecv, dense, packed, chooser, placer, spread,
+    dsend, psend, hsend, hrecv, merged, esend, erecv, gsend, grecv, arranged, late, dense, packed, chooser, placer, spread,
     out_st, out_ch, tri, lower, upper, lenb, bstep, carry,
     acc, tbuf, tstage, tsend, trecv, psum, precv, qsum, qrecv, tot,
-    load_sem, meta_sem, own_sem, ds_sem, dr_sem, ks_sem, kr_sem, hs_sem, hr_sem, fs_sem, xs_sem, xr_sem, es_sem,
+    load_sem, meta_sem, own_sem, ds_sem, dr_sem, ks_sem, kr_sem, hs_sem, hr_sem, fs_sem, xs_sem, xr_sem, es_sem, er_sem, gs_sem, gr_sem,
     ts_sem, tr_sem, ps_sem, pr_sem, qs_sem, qr_sem,
 ):
     rows, span = rbuf.shape
@@ -163,8 +163,7 @@
     side = me // half
     spot = lax.rem(me, half)
     column = lax.rem(spot, quarter)
-    core = lax.rem(mine, 2)
-    partner = mine + 1 - 2 * core
+    level = spot // quarter
 
     def dp_peer(d):
         return lax.rem(me + d, n_dp)
@@ -176,8 +175,8 @@
         return side * half + lax.rem(me + j, half)
 
     def across(i, f):
-        level = side if f == 0 else 1 - side
-        return (1 - side) * half + level * quarter + lax.rem(column + i, quarter)
+        goal = lax.rem(level + f, 2)
+        return (1 - side) * half + goal * quarter + lax.rem(column + i, quarter)
 
     small = []
     for i, (src, dst) in enumerate(
@@ -227,10 +226,7 @@
             at = slice(c, c + LANES)
             yield at, sum(source[p * piece : (p + 1) * piece, at] * weights[p] for p in range(n_dp))
 
-    def mirrored(key):
-        return jnp.where(key >= own_part, own_part + depth - 1 - key, key)
-
-    core_row = jnp.full((1, LANES), core, jnp.int32)
+    counts = {}
 
     def choose(i, f):
         wanted = jnp.zeros((16, LANES), F32)
@@ -242,22 +238,48 @@
         taken = jnp.max((base + wanted)[0:8], axis=1, keepdims=True)
         base = base.astype(jnp.int32)[0:1]
         wanted = wanted.astype(jnp.int32)[0:1]
-        place = lax.broadcasted_iota(jnp.int32, (depth, LANES), 0)
+        counts[i, f] = base, wanted
+        match_rows(chooser, i, f, own_part, base, wanted)
+        esend[2 * i + f] = jnp.maximum(jnp.broadcast_to(taken, (8, LANES)) - own_part, 0.0)
+
+    def match_rows(target, i, f, size, base, wanted):
+        place = lax.broadcasted_iota(jnp.int32, (size, LANES), 0)
         for v in range(chunks // per_vreg):
             c = lane[0:1] // piece + v * per_vreg
-            key = base + c
-            key = jnp.where(core_row == i, key, mirrored(key))
-            key = jnp.where(c < wanted, key, -1)
+            key = jnp.where(c < wanted, base + c, -1)
             at = slice(v * LANES, (v + 1) * LANES)
-            chooser[i, f, :, at] = (place == key).astype(F32).astype(BF16)
-        return jnp.maximum(jnp.broadcast_to(taken, (8, LANES)) - own_part, 0.0)
+            target[i, f, :, at] = (place == key).astype(F32).astype(BF16)
 
     def pack(x, i, f, source):
-        arranged = jnp.concatenate([part for _, part in pick(across(i, f), source)], axis=0)
-        got = jnp.dot(chooser[i, f], arranged, preferred_element_type=F32).astype(BF16)
-        psend[x, i, f] = got[:own_part]
-        if shared:
-            hsend[x, i, f] = got[own_part:]
+        for c, (_, part) in enumerate(pick(across(i, f), source)):
+            arranged[x, i, f, c * piece : (c + 1) * piece, :] = part
+        psend[x, i, f] = jnp.dot(
+            chooser[i, f], arranged[x, i, f], preferred_element_type=F32
+        ).astype(BF16)
+
+    def ahead(table, own):
+        total = jnp.zeros_like(own)
+        for m in range(n_group):
+            total = total + jnp.where(jnp.full(own.shape, m, jnp.int32) < mine, table[m], 0.0)
+        return total
+
+    def pack_late():
+        for i in range(quarter):
+            for f in range(2 if shared else 0):
+                base, wanted = counts[i, f]
+                skip = ahead(erecv[:, 2 * i + f], esend[2 * i + f])[0:1].astype(jnp.int32)
+                base = base + skip - own_part
+                c = lane[0:1] // piece
+                place = lax.broadcasted_iota(jnp.int32, (shared, LANES), 0)
+                for v in range(chunks // per_vreg):
+                    c = lane[0:1] // piece + v * per_vreg
+                    key = jnp.where(jnp.logical_and(c < wanted, base + c >= skip), base + c, -1)
+                    at = slice(v * LANES, (v + 1) * LANES)
+                    late[:, at] = (place == key).astype(F32).astype(BF16)
+                for x in range(2):
+                    hsend[x, 2 * i + f] = jnp.dot(
+                        late[...], arranged[x, i, f], preferred_element_type=F32
+                    ).astype(BF16)
 
     def copy_dense(x, j, source):
         for at, part in pick(near(j), source):
@@ -286,34 +308,46 @@
 
     last = pl.ds(own_part, shared)
 
-    def swap_copy(x, f):
+    others = range(1, n_group if shared else 1)
+
+    def swap_copy(x, d):
+        k = group_peer(d)
         return remote(
-            hsend.at[x, 1 - core, f], hrecv.at[x, f], xs_sem.at[x, f], xr_sem.at[x, f], (me, partner)
-        )
-
-    def shared_copy(x, f):
+            hsend.at[x, k], hrecv.at[x, mine], xs_sem.at[x, d], xr_sem.at[x, d], (me, k)
+        )
+
+    def shared_copy(x):
         return remote(
-            merged.at[x, f], packed.at[x, spot, last],
-            hs_sem.at[x, f], hr_sem.at[x, spot], (across(core, f), mine),
-        )
-
-    def relay_copy(x, f, own):
-        q = f * quarter + lax.rem(column + core + (0 if own else 1), 2)
+            merged.at[x], packed.at[x, spot, last],
+            hs_sem.at[x], hr_sem.at[x, spot], (across(mine // 2, lax.rem(mine, 2)), mine),
+        )
+
+    def held_by(m):
+        return lax.rem(level + lax.rem(m, 2), 2) * quarter + lax.rem(column + m // 2, 2)
+
+    def relay_copy(x, m, d):
+        q = held_by(m)
         return remote(
             packed.at[x, q, last], packed.at[x, q, last],
-            fs_sem.at[x, f], hr_sem.at[x, q], (me, partner),
+            fs_sem.at[x, d], hr_sem.at[x, q], (me, group_peer(d)),
         )
 
     def swap(x):
-        for f in range(2 if shared else 0):
-            swap_copy(x, f).start()
+        for d in others:
+            swap_copy(x, d).start()
 
     def merge(x):
-        for f in range(2 if shared else 0):
-            swap_copy(x, f).wait_recv()
-            merged[x, f] = hsend[x, core, f] + hrecv[x, f]
-        for f in range(2 if shared else 0):
-            shared_copy(x, f).start()
+        if shared:
+            total = hsend[x, mine]
+            for d in others:
+                swap_copy(x, d).wait_recv()
+            for d in others:
+                total = total + hrecv[x, group_peer(d)]
+            merged[x] = total
+
+    def send_merged(x):
+        if shared:
+            shared_copy(x).start()
 
     def receive_packed(x, part):
         at = pl.ds(*cuts[x][part])
@@ -324,13 +358,14 @@
             ).wait_recv()
 
     def relay(x):
-        for f in range(2 if shared else 0):
-            relay_copy(x, f, True).wait_recv()
-            relay_copy(x, f, True).start()
+        if shared:
+            relay_copy(x, mine, 1).wait_recv()
+        for d in others:
+            relay_copy(x, mine, d).start()
 
     def relayed(x):
-        for f in range(2 if shared else 0):
-            relay_copy(x, f, False).wait_recv()
+        for d in others:
+            relay_copy(x, group_peer(d), 1).wait_recv()
 
     order = []
     for i in range(quarter):
@@ -338,14 +373,13 @@
             order.append(("own", i, f))
             if len(order) < n_dp - 1:
                 order.append(("near", i * 2 + f + 1, 0))
-    beyond_own = {}
 
     def stage(item):
         kind, i, f = item
         if kind == "near":
             copy_dense(0, i, rbuf)
         else:
-            beyond_own[i, f] = choose(i, f)
+            choose(i, f)
             pack(0, i, f, rbuf)
 
     sent = []
@@ -444,28 +478,48 @@
         issue(0, item)
     own = [pltpu.make_async_copy(dsend.at[0, 0], dense.at[0, spot], own_sem.at[0])]
     own[0].start()
-    swap(0)
-    for i in range(quarter):
-        for f in range(2):
-            esend[2 * i + f] = beyond_own[i, f]
+    tells = []
+    for d in range(1, n_group):
+        k = group_peer(d)
+        tells.append(remote(esend, erecv.at[mine], es_sem.at[d], er_sem.at[d], (me, k)))
+        tells[-1].start()
+    erecv[mine] = esend[...]
     for i in range(quarter):
         for f in range(2):
             pack(1, i, f, abuf)
     for j in range(half):
         copy_dense(1, j, abuf)
+    for copy in tells:
+        copy.wait()
+    pack_late()
+    swap(0)
     swap(1)
-    merge(0)
-    tell = remote(esend, erecv, es_sem.at[0], es_sem.at[1], (me, partner))
-    tell.start()
 
     for copy in terms_sent:
         copy.wait()
+    other = 1 - side
+    length = trecv[other * (LANES // piece)]
+    for q in range(1, LANES // piece):
+        length = length + pltpu.roll(trecv[other * (LANES // piece) + q], q * piece, 1)
+    length = jnp.broadcast_to(length[0:1], (16, LANES)).astype(jnp.int32)
+    wanted = used(length)
+    base = jnp.dot(wanted, before, preferred_element_type=F32)
+    alike = (sub // piece == lane // piece).astype(F32).astype(BF16)
+    beyond = jnp.dot(wanted, alike, preferred_element_type=F32)[0:8] - own_part
+    gsend[...] = jnp.maximum(beyond, 0.0)
+    grecv[mine] = gsend[...]
+    for d in range(1, n_group):
+        k = group_peer(d)
+        tells.append(remote(gsend, grecv.at[mine], gs_sem.at[d], gr_sem.at[d], (me, k)))
+        tells[-1].start()
 
     row = sub.astype(F32)
     over = jnp.zeros((8, LANES), F32)
-    tell.wait()
     for slot in range(half):
-        over = jnp.where(esend[slot] + erecv[slot] > shared, 1.0, over)
+        filled = erecv[0, slot]
+        for m in range(1, n_group):
+            filled = filled + erecv[m, slot]
+        over = jnp.where(filled > shared, 1.0, over)
     partial = jnp.where(lax.broadcasted_iota(jnp.int32, (8, LANES), 0) == 5, over, 0.0)
     per_block = LANES // piece
     for b in range(blocks):
@@ -490,7 +544,10 @@
         sums_sent.append(remote(psum, precv.at[me], ps_sem.at[d], pr_sem.at[d], (k, mine)))
         sums_sent[-1].start()
 
-    merge(1)
+    for x in range(2):
+        merge(x)
+    send_merged(0)
+    send_merged(1)
     for item in order:
         issue(1, item)
     own.append(pltpu.make_async_copy(dsend.at[1, 0], dense.at[1, spot], own_sem.at[1]))
@@ -501,22 +558,16 @@
                 sent.append(packed_copy(1, i, f, part))
                 sent[-1].start()
 
-    relay(0)
-    other = 1 - side
-    length = trecv[other * per_block]
-    for s in range(1, per_block):
-        length = length + pltpu.roll(trecv[other * per_block + s], s * piece, 1)
-    length = jnp.broadcast_to(length[0:1], (16, LANES)).astype(jnp.int32)
-    wanted = used(length)
-    base = jnp.dot(wanted, before, preferred_element_type=F32)
+    for copy in tells[n_group - 1 :]:
+        copy.wait()
+    skip = ahead(grecv, gsend[...])
+    skip = jnp.transpose(jnp.broadcast_to(skip[0:1], (LANES, LANES))).astype(jnp.int32)
     base = jnp.transpose(jnp.broadcast_to(base[0:1], (LANES, LANES))).astype(jnp.int32)
     wanted = jnp.transpose(jnp.broadcast_to(wanted.astype(F32)[0:1], (LANES, LANES))).astype(jnp.int32)
 
-    flips = lax.rem(sub // piece + column, 2) != core
-
     def place_chunk(c, _):
         key = base + c
-        key = jnp.where(flips, mirrored(key), key)
+        key = jnp.where(key >= own_part, key + skip, key)
         key = jnp.where(c < wanted, key, -1)
         at = pl.ds(pl.multiple_of(c * piece, piece), piece)
         for n in range(depth // LANES):
@@ -545,6 +596,7 @@
 
     for copy in own[:1] + dense_sent[0]:
         copy.wait()
+    relay(0)
     receive_packed(0, 0)
     relayed(0)
     unpack(0, 0, own_part, True)
@@ -607,8 +659,12 @@
 
     whiten_dense(0, white_r)
     whiten_packed(0, white_r)
-    kept = pltpu.make_async_copy(white_r, white_far.at[pl.ds(0, rows)], own_sem.at[2])
+    rest = rows - white_k.shape[0]
+    kept = pltpu.make_async_copy(
+        white_r.at[pl.ds(0, rest)], white_far.at[pl.ds(0, rest)], own_sem.at[2]
+    )
     kept.start()
+    white_k[...] = white_r[rest:, :]
     for copy in own[1:] + dense_sent[1]:
         copy.wait()
     whiten_dense(1, white_a)
@@ -620,11 +676,11 @@
     whiten_packed(1, white_a)
     for copy in sent:
         copy.wait_send()
-    for x in range(2):
-        for f in range(2 if shared else 0):
-            swap_copy(x, f).wait_send()
-            shared_copy(x, f).wait_send()
-            relay_copy(x, f, True).wait_send()
+    for x in range(2 if shared else 0):
+        shared_copy(x).wait_send()
+        for d in others:
+            swap_copy(x, d).wait_send()
+            relay_copy(x, mine, d).wait_send()
     kept.wait()
 
 
@@ -655,20 +711,24 @@
     parts = len(part_cuts(own_part)[1])
     return pl.pallas_call(
         functools.partial(ragged_kernel, n_dp, n_group, own_part, shared),
-        out_shape=tuple(jax.ShapeDtypeStruct((k * rows, span), BF16) for k in (spare, 1))
+        out_shape=tuple(
+            jax.ShapeDtypeStruct((k, span), BF16) for k in (spare * rows, rows, rows * 5 // 8)
+        )
         + (jax.ShapeDtypeStruct((1,), F32),)
         + (jax.ShapeDtypeStruct((rows, span), BF16),) * 2,
         in_specs=[far] * 7,
-        out_specs=(far, vmem, pl.BlockSpec(memory_space=pltpu.SMEM), far, far),
+        out_specs=(far, vmem, vmem, pl.BlockSpec(memory_space=pltpu.SMEM), far, far),
         scratch_shapes=[
             whole, whole, whole, whole, meta, pltpu.VMEM((blocks, LANES), F32), meta, meta,
             pltpu.VMEM((1, n_dp), jnp.int32),
             dense, pltpu.VMEM((2, half // 2, 2, own_part, LANES), BF16),
-            pltpu.VMEM((2, 2, 2, extra, LANES), BF16),
-            pltpu.VMEM((2, 2, extra, LANES), BF16), pltpu.VMEM((2, 2, extra, LANES), BF16),
-            pltpu.VMEM((half, 8, LANES), F32), pltpu.VMEM((half, 8, LANES), F32),
+            pltpu.VMEM((2, half, extra, LANES), BF16), pltpu.VMEM((2, n_group, extra, LANES), BF16),
+            pltpu.VMEM((2, extra, LANES), BF16),
+            pltpu.VMEM((half, 8, LANES), F32), pltpu.VMEM((n_group, half, 8, LANES), F32),
+            one, pltpu.VMEM((n_group, 8, LANES), F32),
+            pltpu.VMEM((2, 2, 2, chunks, LANES), BF16), pltpu.VMEM((extra, chunks), BF16),
             dense, pltpu.VMEM((2, half, depth, LANES), BF16),
-            pltpu.VMEM((half // 2, 2, depth, chunks), BF16), pltpu.VMEM((half, chunks, depth), BF16),
+            pltpu.VMEM((half // 2, 2, own_part, chunks), BF16), pltpu.VMEM((half, chunks, depth), BF16),
             pltpu.VMEM((2, LANES, span), BF16),
             column, pltpu.VMEM((blocks, LANES, LANES), BF16),
             pltpu.VMEM((wide, wide), BF16), factor, factor,
@@ -678,7 +738,8 @@
             pltpu.VMEM((blocks, 8, LANES), F32),
             dma((2, 4)), dma((5,)), dma((3,)), dma((2, half)), dma((2, half)),
             dma((2, parts, half // 2, 2)), dma((2, parts, half)),
-            dma((2, 2)), dma((2, half)), dma((2, 2)), dma((2, 2)), dma((2, 2)), dma((2,)),
+            dma((2,)), dma((2, half)), dma((2, n_group)), dma((2, n_group)), dma((2, n_group)),
+            dma((n_group,)), dma((n_group,)), dma((n_group,)), dma((n_group,)),
             dma((n_dp,)), dma((n_dp,)), dma((n_dp,)), dma((n_dp,)), dma((n_group,)), dma((n_group,)),
         ],
         compiler_params=pltpu.CompilerParams(
@@ -690,58 +751,50 @@
     )
 
 
-def write_kernel(over, from_r, from_a, whole_r, whole_a, to_r, to_a, bounce, sem):
-    quarter = from_a.shape[0] // 4
-
-    def move(sources, targets):
-        copies = []
-        for x, (src, dst) in enumerate(zip(sources, targets)):
-            for part in range(4):
-                at = pl.ds(part * quarter, quarter)
-                copies.append(pltpu.make_async_copy(src.at[at], dst.at[at], sem.at[x, part]))
-                copies[-1].start()
-        for copy in copies:
-            copy.wait()
+def write_kernel(over, from_r, from_a, from_k, whole_r, whole_a, to_r, to_a, bounce, sem):
+    rows, kept = from_a.shape[0], from_k.shape[0]
+    rest = rows - kept
+
+    def started(src, dst, at):
+        copy = pltpu.make_async_copy(src, dst, sem.at[at])
+        copy.start()
+        return copy
 
     @pl.when(over[0] > 0.0)
     def _():
         for source, target in ((whole_r, to_r), (whole_a, to_a)):
-            move((source,), (bounce,))
-            move((bounce,), (target,))
+            started(source, bounce, 0).wait()
+            started(bounce, target, 0).wait()
 
     @pl.when(jnp.logical_not(over[0] > 0.0))
     def _():
-        reads, writes = [], []
-        for part in range(4):
-            at = pl.ds(part * quarter, quarter)
-            reads.append(pltpu.make_async_copy(from_r.at[at], bounce.at[at], sem.at[2, part]))
-            reads[-1].start()
-        for part in range(4):
-            at = pl.ds(part * quarter, quarter)
-            writes.append(pltpu.make_async_copy(from_a.at[at], to_a.at[at], sem.at[1, part]))
-            writes[-1].start()
-        for part in range(4):
-            at = pl.ds(part * quarter, quarter)
-            reads[part].wait()
-            writes.append(pltpu.make_async_copy(bounce.at[at], to_r.at[at], sem.at[0, part]))
-            writes[-1].start()
+        half = rest // 2
+        parts = [pl.ds(half * k, half) for k in range(2)]
+        reads = [started(from_r.at[at], bounce.at[at], k) for k, at in enumerate(parts)]
+        writes = [started(from_k, to_r.at[pl.ds(rest, kept)], 2)]
+        for k in range(2):
+            at = pl.ds(k * rows // 2, rows // 2)
+            writes.append(started(from_a.at[at], to_a.at[at], 3 + k))
+        for k, at in enumerate(parts):
+            reads[k].wait()
+            writes.append(started(bounce.at[at], to_r.at[at], 5 + k))
         for copy in writes:
             copy.wait()
 
 
-def write(over, packed_way, whole_way):
+def write(over, results, whole_way):
     vmem = pl.BlockSpec(memory_space=pltpu.VMEM)
     far = pl.BlockSpec(memory_space=pltpu.HBM)
-    shape = packed_way[1].shape
+    shape = whole_way[0].shape
     return tuple(
         pl.pallas_call(
             write_kernel,
             out_shape=[jax.ShapeDtypeStruct(x.shape, x.dtype) for x in whole_way],
-            in_specs=[pl.BlockSpec(memory_space=pltpu.SMEM), far, vmem, far, far],
+            in_specs=[pl.BlockSpec(memory_space=pltpu.SMEM), far, vmem, vmem, far, far],
             out_specs=[far, far],
-            scratch_shapes=[pltpu.VMEM(shape, BF16), pltpu.SemaphoreType.DMA((3, 4))],
+            scratch_shapes=[pltpu.VMEM(shape, BF16), pltpu.SemaphoreType.DMA((7,))],
             compiler_params=pltpu.CompilerParams(vmem_limit_bytes=52_000_000),
-        )(over, *packed_way, *whole_way)
+        )(over, *results, *whole_way)
     )
 
 
@@ -752,24 +805,26 @@
     args = (rewards, values, lengths, decay_rate, piece_dest, row_perm, minibatch)
     if piece % 16 or LANES % piece or block != LANES or span % 4096:
         return plain_local(*args)
-    if n_dp // 4 != 2 or n_dp % 4 or n_group % 2 or blocks != 2 or n_dp // 2 * piece != LANES:
+    if n_dp // 4 != 2 or n_dp % 4 or n_group != 4 or blocks != 2 or n_dp // 2 * piece != LANES:
         return plain_local(*args)
     chunks = piece * (span // LANES)
-    own_part, shared = chunks * 9 // 16, chunks * 3 // 16
+    own_part, shared = chunks * 36 // 64, chunks * 12 // 64
 
     def whole(results):
-        return results[0][:rows], results[1]
-
-    white_rewards, white_advantage, over, *unused = ragged(
+        kept = results[2]
+        rest = rows - kept.shape[0]
+        return jnp.concatenate([results[0][:rest], kept], axis=0), results[1]
+
+    *results, over, unused_r, unused_a = ragged(
         n_dp, n_group, own_part, shared, 0, 8, *args
     )
     whole_way = lax.cond(
         over[0] > 0.0,
         lambda unused, args: whole(ragged(n_dp, n_group, chunks, 0, 1, 1, *args)),
         lambda unused, args: tuple(unused),
-        unused, args,
-    )
-    return write(over, (white_rewards, white_advantage), whole_way)
+        (unused_r, unused_a), args,
+    )
+    return write(over, results, whole_way)
 
 
 def solution(mesh):

time: 80.7 us -> 75.1 us (0.931)
  Pallas kernels: 78.7 us -> 73.1 us
    pallas_call x1, Pallas kernels: 74.8 us -> 70 us  [ragged(): pl.pallas_call(functools.partial(ragged_kernel, n_dp, n_group, own_part,...]
where the time goes in v4:
time: 75.1 us; the launch traced here: 74.9 us
  Pallas kernels  73.1 us (97%)
  between operations  1.55 us (2%)
    pallas_call x1, Pallas kernels, ragged(): pl.pallas_call(functools.partial(ragged_kernel, n_dp, n_group, own_part,...  70 us
    pallas_call x1, Pallas kernels, write(): pl.pallas_call(write_kernel, out_shape=[jax.ShapeDtypeStruct(x.shape, x.d...  3.09 us

profile of v4, /device:TPU:0, one launch (start us, length us, event | category | flops | bytes accessed | tf_op | source)
XLA Modules:
  0.0 74.9 jit_solution(8439358092859568285)
XLA Ops:
  0.6 0.0 copy-start
  0.6 0.0 copy-start.1
  0.7 0.0 copy-start.2
  0.7 0.0 copy-start.3
  0.7 0.0 copy-start.4
  0.7 70.0 %shard_map.86 = (bf16[2048,4096]{1,0:T(8,128)(2,1)}, bf16[256,4096]{1,0:T(8,128)(2,1)S(1)}, bf16[160,4096]{1,0:T(8,128)(2,1)S(1)}, f32[1]{0:T(128)}, bf16[256,40...) custom-call(bf16[256,4096]{1,0:T(8,128)(2,1)} %rew_hbm.1, bf16[256,4096]{1,0:T(8,128)(2,1)} %val_hbm.1, s32[2,128]{1,0:T(2,128)} %bitcast.7, ...), custom_call_target="tpu_custom_call" | custom-call | tf_op jit(solution)/shard_map/pallas_call | solution.py:712
  71.3 0.0 copy-done
  71.3 0.0 copy-done.1
  71.3 0.0 copy-done.2
  71.3 0.0 copy-done.3
  71.3 0.0 copy-done.4
  71.3 0.3 conditional.1
  71.6 3.1 %shard_map.87 = (bf16[256,4096]{1,0:T(8,128)(2,1)}, bf16[256,4096]{1,0:T(8,128)(2,1)}) custom-call(f32[1]{0:T(128)} %get-tuple-element.38.over, bf16[2048,4096]{1,0:T(8,128)(2,1)} %get-tuple-element.39.from_r, bf16[256,4096]{1,0:T(8,128)(2,1)S(1)} %get-tuple-element.40.from_a, bf16[160,4096]{1,0:T(8,128)(2,1)S(1)} %get-tuple-element.41.from_k, ...), custom_call_target="tpu_custom_call" | custom-call | tf_op jit(solution)/shard_map/pallas_call | solution.py:790
Async XLA Ops:
  0.6 70.7 %copy-start = (s32[256]{0:T(256)S(1)}, s32[256]{0:T(256)}, u32[]{:S(2)}) copy-start(s32[256]{0:T(256)} %param.11) | copy-start | bytes 3076
  0.6 70.7 %copy-start.1 = (f32[256]{0:T(256)S(1)}, f32[256]{0:T(256)}, u32[]{:S(2)}) copy-start(f32[256]{0:T(256)} %param.12) | copy-start | bytes 3076
  0.7 70.7 %copy-start.2 = (s32[2,128]{1,0:T(2,128)S(1)}, s32[2,128]{1,0:T(2,128)}, u32[]{:S(2)}) copy-start(s32[2,128]{1,0:T(2,128)} %perm_hbm.1) | copy-start | bytes 3076
  0.7 70.7 %copy-start.3 = (s32[256]{0:T(256)S(1)}, s32[256]{0:T(256)}, u32[]{:S(2)}) copy-start(s32[256]{0:T(256)} %param.15) | copy-start | bytes 3076
  0.7 70.7 %copy-start.4 = (s32[1,8]{1,0:T(1,128)S(1)}, s32[1,8]{1,0:T(1,128)}, u32[]{:S(2)}) copy-start(s32[1,8]{1,0:T(1,128)} %dest_hbm.1) | copy-start | bytes 100

commit v5 on v4

--- a/solution.py
+++ b/solution.py
@@ -143,7 +143,7 @@
     rew_hbm, val_hbm, len_hbm, rate_hbm, dest_hbm, perm_hbm, mini_hbm,
     white_far, white_a, white_k, over_out, unused_r, unused_a,
     rbuf, vbuf, abuf, white_r, len_v, rate_v, perm_v, mini_v, dest_v,
-    dsend, psend, hsend, hrecv, merged, esend, erecv, gsend, grecv, arranged, late, dense, packed, chooser, placer, spread,
+    dsend, psend, hsend, hrecv, merged, esend, erecv, gsend, grecv, arranged, late, flag_v, dense, packed, chooser, placer, spread,
     out_st, out_ch, tri, lower, upper, lenb, bstep, carry,
     acc, tbuf, tstage, tsend, trecv, psum, precv, qsum, qrecv, tot,
     load_sem, meta_sem, own_sem, ds_sem, dr_sem, ks_sem, kr_sem, hs_sem, hr_sem, fs_sem, xs_sem, xr_sem, es_sem, er_sem, gs_sem, gr_sem,
@@ -592,7 +592,7 @@
                 spread[x, at, cols] = part if first else spread[x, at, cols] + part
             return 0
 
-        lax.fori_loop(0, half, one, 0)
+        lax.fori_loop(0, half, one, 0, unroll=2)
 
     for copy in own[:1] + dense_sent[0]:
         copy.wait()
@@ -619,7 +619,9 @@
     total = qrecv[0]
     for k in range(1, n_group):
         total = total + qrecv[k]
-    over_out[0] = jnp.max(total[5:6, :])
+    flag_v[...] = jnp.full((8, LANES), jnp.max(total[5:6, :]))
+    flag_copy = pltpu.make_async_copy(flag_v, over_out, own_sem.at[3])
+    flag_copy.start()
 
     count = jnp.maximum(total[0:1, :], 1.0)
     means = total[1:3, :] / count
@@ -636,7 +638,7 @@
         out_st[at, :] = jnp.transpose(here)
 
     def whiten_block(x, arrived_at, b, target):
-        tile = 512
+        tile = 1024
 
         def tile_step(i, _):
             col = pl.multiple_of(i * tile, tile)
@@ -649,7 +651,7 @@
             target[at, pl.ds(col, tile)] = white.astype(BF16)
             return 0
 
-        lax.fori_loop(0, span // tile, tile_step, 0)
+        lax.fori_loop(0, span // tile, tile_step, 0, unroll=2)
 
     def whiten_dense(x, target):
         whiten_block(x, lambda at: dense[x, :, :, at].reshape(LANES, at.size), side, target)
@@ -682,11 +684,12 @@
             swap_copy(x, d).wait_send()
             relay_copy(x, mine, d).wait_send()
     kept.wait()
+    flag_copy.wait()
 
 
 def part_cuts(size):
-    a, b = size // 256 * 128, (size - 1) // 128 * 128
-    return (((0, size),), ((0, a), (a, b - a), (b, size - b)))
+    b = (size - 1) // 128 * 128
+    return (((0, size),), ((0, b), (b, size - b)))
 
 
 def ragged(n_dp, n_group, own_part, shared, collective_id, spare, rewards, values, lengths, decay_rate, piece_dest, row_perm, minibatch):
@@ -714,10 +717,10 @@
         out_shape=tuple(
             jax.ShapeDtypeStruct((k, span), BF16) for k in (spare * rows, rows, rows * 5 // 8)
         )
-        + (jax.ShapeDtypeStruct((1,), F32),)
+        + (jax.ShapeDtypeStruct((8, LANES), F32),)
         + (jax.ShapeDtypeStruct((rows, span), BF16),) * 2,
         in_specs=[far] * 7,
-        out_specs=(far, vmem, vmem, pl.BlockSpec(memory_space=pltpu.SMEM), far, far),
+        out_specs=(far, vmem, vmem, far, far, far),
         scratch_shapes=[
             whole, whole, whole, whole, meta, pltpu.VMEM((blocks, LANES), F32), meta, meta,
             pltpu.VMEM((1, n_dp), jnp.int32),
@@ -726,7 +729,7 @@
             pltpu.VMEM((2, extra, LANES), BF16),
             pltpu.VMEM((half, 8, LANES), F32), pltpu.VMEM((n_group, half, 8, LANES), F32),
             one, pltpu.VMEM((n_group, 8, LANES), F32),
-            pltpu.VMEM((2, 2, 2, chunks, LANES), BF16), pltpu.VMEM((extra, chunks), BF16),
+            pltpu.VMEM((2, 2, 2, chunks, LANES), BF16), pltpu.VMEM((extra, chunks), BF16), one,
             dense, pltpu.VMEM((2, half, depth, LANES), BF16),
             pltpu.VMEM((half // 2, 2, own_part, chunks), BF16), pltpu.VMEM((half, chunks, depth), BF16),
             pltpu.VMEM((2, LANES, span), BF16),
@@ -736,7 +739,7 @@
             pltpu.VMEM((4, rows, LANES), F32), column, pltpu.VMEM((LANES, LANES), F32),
             small, small, one, small, one, pltpu.VMEM((n_group, 8, LANES), F32),
             pltpu.VMEM((blocks, 8, LANES), F32),
-            dma((2, 4)), dma((5,)), dma((3,)), dma((2, half)), dma((2, half)),
+            dma((2, 4)), dma((5,)), dma((4,)), dma((2, half)), dma((2, half)),
             dma((2, parts, half // 2, 2)), dma((2, parts, half)),
             dma((2,)), dma((2, half)), dma((2, n_group)), dma((2, n_group)), dma((2, n_group)),
             dma((n_group,)), dma((n_group,)), dma((n_group,)), dma((n_group,)),
@@ -751,7 +754,9 @@
     )
 
 
-def write_kernel(over, from_r, from_a, from_k, whole_r, whole_a, to_r, to_a, bounce, sem):
+def write_kernel(
+    over_far, from_r, from_a, from_k, whole_r, whole_a, to_r, to_a, bounce, over, sem
+):
     rows, kept = from_a.shape[0], from_k.shape[0]
     rest = rows - kept
 
@@ -760,26 +765,27 @@
         copy.start()
         return copy
 
-    @pl.when(over[0] > 0.0)
+    flag = started(over_far, over, 0)
+    half = rest // 2
+    parts = [pl.ds(half * k, half) for k in range(2)]
+    reads = [started(from_r.at[at], bounce.at[at], 1 + k) for k, at in enumerate(parts)]
+    writes = []
+    for k in range(2):
+        at = pl.ds(k * rows // 2, rows // 2)
+        writes.append(started(from_a.at[at], to_a.at[at], 3 + k))
+    writes.append(started(from_k, to_r.at[pl.ds(rest, kept)], 5))
+    for k, at in enumerate(parts):
+        reads[k].wait()
+        writes.append(started(bounce.at[at], to_r.at[at], 6 + k))
+    flag.wait()
+    for copy in writes:
+        copy.wait()
+
+    @pl.when(jnp.max(over[...]) > 0.0)
     def _():
         for source, target in ((whole_r, to_r), (whole_a, to_a)):
-            started(source, bounce, 0).wait()
-            started(bounce, target, 0).wait()
-
-    @pl.when(jnp.logical_not(over[0] > 0.0))
-    def _():
-        half = rest // 2
-        parts = [pl.ds(half * k, half) for k in range(2)]
-        reads = [started(from_r.at[at], bounce.at[at], k) for k, at in enumerate(parts)]
-        writes = [started(from_k, to_r.at[pl.ds(rest, kept)], 2)]
-        for k in range(2):
-            at = pl.ds(k * rows // 2, rows // 2)
-            writes.append(started(from_a.at[at], to_a.at[at], 3 + k))
-        for k, at in enumerate(parts):
-            reads[k].wait()
-            writes.append(started(bounce.at[at], to_r.at[at], 5 + k))
-        for copy in writes:
-            copy.wait()
+            started(source, bounce, 1).wait()
+            started(bounce, target, 1).wait()
 
 
 def write(over, results, whole_way):
@@ -790,9 +796,11 @@
         pl.pallas_call(
             write_kernel,
             out_shape=[jax.ShapeDtypeStruct(x.shape, x.dtype) for x in whole_way],
-            in_specs=[pl.BlockSpec(memory_space=pltpu.SMEM), far, vmem, vmem, far, far],
+            in_specs=[far, far, vmem, vmem, far, far],
             out_specs=[far, far],
-            scratch_shapes=[pltpu.VMEM(shape, BF16), pltpu.SemaphoreType.DMA((7,))],
+            scratch_shapes=[
+                pltpu.VMEM(shape, BF16), pltpu.VMEM(over.shape, F32), pltpu.SemaphoreType.DMA((8,)),
+            ],
             compiler_params=pltpu.CompilerParams(vmem_limit_bytes=52_000_000),
         )(over, *results, *whole_way)
     )
@@ -819,7 +827,7 @@
         n_dp, n_group, own_part, shared, 0, 8, *args
     )
     whole_way = lax.cond(
-        over[0] > 0.0,
+        over[0, 0] > 0.0,
         lambda unused, args: whole(ragged(n_dp, n_group, chunks, 0, 1, 1, *args)),
         lambda unused, args: tuple(unused),
         (unused_r, unused_a), args,

time: 75.1 us -> 73.1 us (0.973)
  Pallas kernels: 73.1 us -> 70.8 us
    pallas_call x1, Pallas kernels: 70 us -> 68.2 us  [ragged(): pl.pallas_call(functools.partial(ragged_kernel, n_dp, n_group, own_part,...]
where the time goes in v5:
time: 73.1 us; the launch traced here: 72.9 us
  Pallas kernels  70.8 us (97%)
  between operations  1.54 us (2%)
    pallas_call x1, Pallas kernels, ragged(): pl.pallas_call(functools.partial(ragged_kernel, n_dp, n_group, own_part,...  68.2 us
    pallas_call x1, Pallas kernels, write(): pl.pallas_call(write_kernel, out_shape=[jax.ShapeDtypeStruct(x.shape, x.d...  2.6 us

profile of v5, /device:TPU:0, one launch (start us, length us, event | category | flops | bytes accessed | tf_op | source)
XLA Modules:
  0.0 72.9 jit_solution(5634925962828516568)
XLA Ops:
  0.6 0.0 copy-start
  0.6 0.0 copy-start.1
  0.7 0.0 copy-start.2
  0.7 0.0 copy-start.3
  0.7 0.0 copy-start.4
  0.7 68.2 %shard_map.86 = (bf16[2048,4096]{1,0:T(8,128)(2,1)}, bf16[256,4096]{1,0:T(8,128)(2,1)S(1)}, bf16[160,4096]{1,0:T(8,128)(2,1)S(1)}, f32[8,128]{1,0:T(8,128)S(1)},...) custom-call(bf16[256,4096]{1,0:T(8,128)(2,1)} %rew_hbm.1, bf16[256,4096]{1,0:T(8,128)(2,1)} %val_hbm.1, ...), custom_call_target="tpu_custom_call" | custom-call | tf_op jit(solution)/shard_map/pallas_call | solution.py:715
  68.9 0.5 slice.6
  70.1 0.0 copy-done
  70.1 0.0 copy-done.1
  70.1 0.0 copy-done.2
  70.1 0.0 copy-done.3
  70.1 0.0 copy-done.4
  70.1 2.6 %shard_map.87 = (bf16[256,4096]{1,0:T(8,128)(2,1)}, bf16[256,4096]{1,0:T(8,128)(2,1)}) custom-call(f32[8,128]{1,0:T(8,128)S(1)} %get-tuple-element.38.over_far, bf16[2048,4096]{1,0:T(8,128)(2,1)} %get-tuple-element.39.from_r, bf16[256,4096]{1,0:T(8,128)(2,1)S(1)} %get-tuple-element.40.from_a, bf16[160,4096]{1,0:T(8,128)(2,1)S(1)} %get-tuple-element.41.from_k, ...), custom_call_target="tpu_custom_call" | custom-call | tf_op jit(solution)/shard_map/pallas_call | solution.py:796
  (1 shorter events, 0.0 us)
Async XLA Ops:
  0.6 69.5 %copy-start = (s32[256]{0:T(256)S(1)}, s32[256]{0:T(256)}, u32[]{:S(2)}) copy-start(s32[256]{0:T(256)} %param.11) | copy-start | bytes 3076
  0.6 69.5 %copy-start.1 = (f32[256]{0:T(256)S(1)}, f32[256]{0:T(256)}, u32[]{:S(2)}) copy-start(f32[256]{0:T(256)} %param.12) | copy-start | bytes 3076
  0.7 69.5 %copy-start.2 = (s32[2,128]{1,0:T(2,128)S(1)}, s32[2,128]{1,0:T(2,128)}, u32[]{:S(2)}) copy-start(s32[2,128]{1,0:T(2,128)} %perm_hbm.1) | copy-start | bytes 3076
  0.7 69.5 %copy-start.3 = (s32[256]{0:T(256)S(1)}, s32[256]{0:T(256)}, u32[]{:S(2)}) copy-start(s32[256]{0:T(256)} %param.15) | copy-start | bytes 3076
  0.7 69.5 %copy-start.4 = (s32[1,8]{1,0:T(1,128)S(1)}, s32[1,8]{1,0:T(1,128)}, u32[]{:S(2)}) copy-start(s32[1,8]{1,0:T(1,128)} %dest_hbm.1) | copy-start | bytes 100
